TPU v7x, 32 devices: a 4x4x1 block of a 4x4x8 slice. The times are simulated.
32 devices in a mesh: dp: 1 (over z), cp: 32 (over y, x, core).
Axes of the slice: x: 4, y: 4, z: 1, core: 2. Of those that a mesh axis runs over, the one named last changes fastest.
The devices are a block of a 4x4x8 slice.
Arguments:
- q_tok: bfloat16 [32768, 2, 128], P(('dp', 'cp'))
- k_tok: bfloat16 [32768, 128], P(('dp', 'cp'))
- v_tok: bfloat16 [32768, 128], P(('dp', 'cp'))
- fwd_out: bfloat16 [32768, 2, 128], P(('dp', 'cp'))
- d_out: bfloat16 [32768, 2, 128], P(('dp', 'cp'))
- lse_row: float32 [32768, 2], P(('dp', 'cp'))
Outputs:
- output 1: bfloat16 [32768, 2, 128], P(('dp', 'cp'))
- output 2: bfloat16 [32768, 128], P(('dp', 'cp'))
- output 3: bfloat16 [32768, 128], P(('dp', 'cp'))
All inputs are finite; a program needn't handle non-finite values.
Results may differ from a plain program's by a relative error of at most 0.001.
Values are sent between devices in bfloat16 or wider.
A program may use at most 768 MiB of HBM per device.

v0:
```python
import jax
import jax.numpy as jnp
from jax import lax
from jax.sharding import PartitionSpec as P


def pair_scores(q_block, do_block, lse_block, delta_block, k_block, v_block, on_diag, softmax_scale):
    logits = jnp.einsum('rgd,cd->rgc', q_block, k_block, preferred_element_type=jnp.float32)
    row_ids = jnp.arange(q_block.shape[0])
    allowed = jnp.logical_or(row_ids[None, :] <= row_ids[:, None], jnp.logical_not(on_diag))
    prob_mat = jnp.exp(jnp.where(allowed[:, None, :], logits * softmax_scale - lse_block[:, :, None], -jnp.inf))
    d_prob = jnp.einsum('rgd,cd->rgc', do_block, v_block, preferred_element_type=jnp.float32)
    d_score = (prob_mat * (d_prob - delta_block[:, :, None])).astype(jnp.bfloat16)
    return prob_mat.astype(jnp.bfloat16), d_score


def solution(mesh):
    n_dev = mesh.shape['cp']
    forward_perm = [(i, (i + 1) % n_dev) for i in range(n_dev)]
    row_spec = P(('dp', 'cp'))

    def local_fn(q_tok, k_tok, v_tok, fwd_out, d_out, lse_row):
        softmax_scale = q_tok.shape[-1] ** -0.5
        my_index = lax.axis_index('cp')
        row_delta = jnp.einsum('rgd,rgd->rg', d_out, fwd_out, preferred_element_type=jnp.float32)

        def accumulate(step, state):
            def pair_update(state_in):
                dq_acc, k_cur, v_cur, dk_acc, dv_acc = state_in
                prob_low, score_low = pair_scores(q_tok, d_out, lse_row, row_delta, k_cur, v_cur, step == 0, softmax_scale)
                dq_acc = dq_acc + jnp.einsum('rgc,cd->rgd', score_low, k_cur, preferred_element_type=jnp.float32)
                dk_acc = dk_acc + jnp.einsum('rgc,rgd->cd', score_low, q_tok, preferred_element_type=jnp.float32)
                dv_acc = dv_acc + jnp.einsum('rgc,rgd->cd', prob_low, d_out, preferred_element_type=jnp.float32)
                return (dq_acc, k_cur, v_cur, dk_acc, dv_acc)

            def keep_state(state_in):
                return state_in

            return lax.cond(step <= my_index, pair_update, keep_state, state)

        def step_fn(step, state):
            dq_acc, k_cur, v_cur, dk_acc, dv_acc = accumulate(step, state)
            k_next = lax.ppermute(k_cur, 'cp', forward_perm)
            v_next = lax.ppermute(v_cur, 'cp', forward_perm)
            dk_next = lax.ppermute(dk_acc, 'cp', forward_perm)
            dv_next = lax.ppermute(dv_acc, 'cp', forward_perm)
            return (dq_acc, k_next, v_next, dk_next, dv_next)

        kv_zeros = jnp.zeros(k_tok.shape, jnp.float32)
        state = (jnp.zeros(q_tok.shape, jnp.float32), k_tok, v_tok, kv_zeros, kv_zeros)
        state = lax.fori_loop(0, n_dev - 1, step_fn, state)
        dq_acc, k_cur, v_cur, dk_acc, dv_acc = accumulate(n_dev - 1, state)
        dk_home = lax.ppermute(dk_acc, 'cp', forward_perm)
        dv_home = lax.ppermute(dv_acc, 'cp', forward_perm)
        grad_q = (dq_acc * softmax_scale).astype(jnp.bfloat16)
        grad_k = (dk_home * softmax_scale).astype(jnp.bfloat16)
        grad_v = dv_home.astype(jnp.bfloat16)
        return grad_q, grad_k, grad_v

    return jax.shard_map(local_fn, mesh=mesh, in_specs=(row_spec, row_spec, row_spec, row_spec, row_spec, row_spec), out_specs=(row_spec, row_spec, row_spec), check_vma=False)
```

profile of v0, /device:TPU:126, one launch (start us, length us, event | category | flops | bytes accessed | tf_op | source)
XLA Modules:
  0.0 1078.5 jit_solution(12888817641755851025)
XLA Ops:
  9.1 1055.5 %while.21 = (s32[]{:T(128)}, f32[1024,2,128]{2,0,1:T(8,128)S(1)}, bf16[1024,128]{1,0:T(8,128)(2,1)S(1)}, bf16[1024,128]{1,0:T(8,128)(2,1)S(1)}, f32[1024,128]{1,...) while((s32[]{:T(128)}, f32[1024,2,128]{2,0,1:T(8,128)S(1)}, ...), condition=%wide.region_3.4_spmd, body=%wide.region_0.3_spmd.sunk | while | flops 2707947520 | bytes 57467344 | solution.py:51
  9.8 13.4 %conditional.4 = ((f32[1024,2,128]{2,0,1:T(8,128)S(1)}, f32[1024,128]{1,0:T(8,128)S(1)}, f32[1024,128]{1,0:T(8,128)})) conditional(s32[]{:T(128)} %convert_element_type.52, (f32[1024,2,128]{2,0,1:T(8,128)S(1)}, f32[1024,128]{1,0:T(8,128)S(1)}, f32[1024,128]{1,0:T(8,128)}) %tuple.54, (s32[]{:T(128)}, bf16[1024,2,128]{2,0,1:T(8,128)(2,1)S(1)}, ...), branch_computations={%region_1.0_spmd, %region_2.2_spmd} | conditional | flops 2707947520 | bytes 48029768 | solution.py:39
  43.9 13.4 %conditional.4 = ((f32[1024,2,128]{2,0,1:T(8,128)S(1)}, f32[1024,128]{1,0:T(8,128)S(1)}, f32[1024,128]{1,0:T(8,128)})) conditional(s32[]{:T(128)} %convert_element_type.52, (f32[1024,2,128]{2,0,1:T(8,128)S(1)}, f32[1024,128]{1,0:T(8,128)S(1)}, f32[1024,128]{1,0:T(8,128)}) %tuple.54, (s32[]{:T(128)}, bf16[1024,2,128]{2,0,1:T(8,128)(2,1)S(1)}, ...), branch_computations={%region_1.0_spmd, %region_2.2_spmd} | conditional | flops 2707947520 | bytes 48029768 | solution.py:39
  77.9 13.4 %conditional.4 = ((f32[1024,2,128]{2,0,1:T(8,128)S(1)}, f32[1024,128]{1,0:T(8,128)S(1)}, f32[1024,128]{1,0:T(8,128)})) conditional(s32[]{:T(128)} %convert_element_type.52, (f32[1024,2,128]{2,0,1:T(8,128)S(1)}, f32[1024,128]{1,0:T(8,128)S(1)}, f32[1024,128]{1,0:T(8,128)}) %tuple.54, (s32[]{:T(128)}, bf16[1024,2,128]{2,0,1:T(8,128)(2,1)S(1)}, ...), branch_computations={%region_1.0_spmd, %region_2.2_spmd} | conditional | flops 2707947520 | bytes 48029768 | solution.py:39
  112.0 13.4 %conditional.4 = ((f32[1024,2,128]{2,0,1:T(8,128)S(1)}, f32[1024,128]{1,0:T(8,128)S(1)}, f32[1024,128]{1,0:T(8,128)})) conditional(s32[]{:T(128)} %convert_element_type.52, (f32[1024,2,128]{2,0,1:T(8,128)S(1)}, f32[1024,128]{1,0:T(8,128)S(1)}, f32[1024,128]{1,0:T(8,128)}) %tuple.54, (s32[]{:T(128)}, bf16[1024,2,128]{2,0,1:T(8,128)(2,1)S(1)}, ...), branch_computations={%region_1.0_spmd, %region_2.2_spmd} | conditional | flops 2707947520 | bytes 48029768 | solution.py:39
  146.0 13.4 %conditional.4 = ((f32[1024,2,128]{2,0,1:T(8,128)S(1)}, f32[1024,128]{1,0:T(8,128)S(1)}, f32[1024,128]{1,0:T(8,128)})) conditional(s32[]{:T(128)} %convert_element_type.52, (f32[1024,2,128]{2,0,1:T(8,128)S(1)}, f32[1024,128]{1,0:T(8,128)S(1)}, f32[1024,128]{1,0:T(8,128)}) %tuple.54, (s32[]{:T(128)}, bf16[1024,2,128]{2,0,1:T(8,128)(2,1)S(1)}, ...), branch_computations={%region_1.0_spmd, %region_2.2_spmd} | conditional | flops 2707947520 | bytes 48029768 | solution.py:39
  180.1 13.4 %conditional.4 = ((f32[1024,2,128]{2,0,1:T(8,128)S(1)}, f32[1024,128]{1,0:T(8,128)S(1)}, f32[1024,128]{1,0:T(8,128)})) conditional(s32[]{:T(128)} %convert_element_type.52, (f32[1024,2,128]{2,0,1:T(8,128)S(1)}, f32[1024,128]{1,0:T(8,128)S(1)}, f32[1024,128]{1,0:T(8,128)}) %tuple.54, (s32[]{:T(128)}, bf16[1024,2,128]{2,0,1:T(8,128)(2,1)S(1)}, ...), branch_computations={%region_1.0_spmd, %region_2.2_spmd} | conditional | flops 2707947520 | bytes 48029768 | solution.py:39
  214.1 13.4 %conditional.4 = ((f32[1024,2,128]{2,0,1:T(8,128)S(1)}, f32[1024,128]{1,0:T(8,128)S(1)}, f32[1024,128]{1,0:T(8,128)})) conditional(s32[]{:T(128)} %convert_element_type.52, (f32[1024,2,128]{2,0,1:T(8,128)S(1)}, f32[1024,128]{1,0:T(8,128)S(1)}, f32[1024,128]{1,0:T(8,128)}) %tuple.54, (s32[]{:T(128)}, bf16[1024,2,128]{2,0,1:T(8,128)(2,1)S(1)}, ...), branch_computations={%region_1.0_spmd, %region_2.2_spmd} | conditional | flops 2707947520 | bytes 48029768 | solution.py:39
  248.2 13.4 %conditional.4 = ((f32[1024,2,128]{2,0,1:T(8,128)S(1)}, f32[1024,128]{1,0:T(8,128)S(1)}, f32[1024,128]{1,0:T(8,128)})) conditional(s32[]{:T(128)} %convert_element_type.52, (f32[1024,2,128]{2,0,1:T(8,128)S(1)}, f32[1024,128]{1,0:T(8,128)S(1)}, f32[1024,128]{1,0:T(8,128)}) %tuple.54, (s32[]{:T(128)}, bf16[1024,2,128]{2,0,1:T(8,128)(2,1)S(1)}, ...), branch_computations={%region_1.0_spmd, %region_2.2_spmd} | conditional | flops 2707947520 | bytes 48029768 | solution.py:39
  282.2 13.4 %conditional.4 = ((f32[1024,2,128]{2,0,1:T(8,128)S(1)}, f32[1024,128]{1,0:T(8,128)S(1)}, f32[1024,128]{1,0:T(8,128)})) conditional(s32[]{:T(128)} %convert_element_type.52, (f32[1024,2,128]{2,0,1:T(8,128)S(1)}, f32[1024,128]{1,0:T(8,128)S(1)}, f32[1024,128]{1,0:T(8,128)}) %tuple.54, (s32[]{:T(128)}, bf16[1024,2,128]{2,0,1:T(8,128)(2,1)S(1)}, ...), branch_computations={%region_1.0_spmd, %region_2.2_spmd} | conditional | flops 2707947520 | bytes 48029768 | solution.py:39
  316.2 13.4 %conditional.4 = ((f32[1024,2,128]{2,0,1:T(8,128)S(1)}, f32[1024,128]{1,0:T(8,128)S(1)}, f32[1024,128]{1,0:T(8,128)})) conditional(s32[]{:T(128)} %convert_element_type.52, (f32[1024,2,128]{2,0,1:T(8,128)S(1)}, f32[1024,128]{1,0:T(8,128)S(1)}, f32[1024,128]{1,0:T(8,128)}) %tuple.54, (s32[]{:T(128)}, bf16[1024,2,128]{2,0,1:T(8,128)(2,1)S(1)}, ...), branch_computations={%region_1.0_spmd, %region_2.2_spmd} | conditional | flops 2707947520 | bytes 48029768 | solution.py:39
  350.3 13.4 %conditional.4 = ((f32[1024,2,128]{2,0,1:T(8,128)S(1)}, f32[1024,128]{1,0:T(8,128)S(1)}, f32[1024,128]{1,0:T(8,128)})) conditional(s32[]{:T(128)} %convert_element_type.52, (f32[1024,2,128]{2,0,1:T(8,128)S(1)}, f32[1024,128]{1,0:T(8,128)S(1)}, f32[1024,128]{1,0:T(8,128)}) %tuple.54, (s32[]{:T(128)}, bf16[1024,2,128]{2,0,1:T(8,128)(2,1)S(1)}, ...), branch_computations={%region_1.0_spmd, %region_2.2_spmd} | conditional | flops 2707947520 | bytes 48029768 | solution.py:39
  384.3 13.4 %conditional.4 = ((f32[1024,2,128]{2,0,1:T(8,128)S(1)}, f32[1024,128]{1,0:T(8,128)S(1)}, f32[1024,128]{1,0:T(8,128)})) conditional(s32[]{:T(128)} %convert_element_type.52, (f32[1024,2,128]{2,0,1:T(8,128)S(1)}, f32[1024,128]{1,0:T(8,128)S(1)}, f32[1024,128]{1,0:T(8,128)}) %tuple.54, (s32[]{:T(128)}, bf16[1024,2,128]{2,0,1:T(8,128)(2,1)S(1)}, ...), branch_computations={%region_1.0_spmd, %region_2.2_spmd} | conditional | flops 2707947520 | bytes 48029768 | solution.py:39
  418.4 13.4 %conditional.4 = ((f32[1024,2,128]{2,0,1:T(8,128)S(1)}, f32[1024,128]{1,0:T(8,128)S(1)}, f32[1024,128]{1,0:T(8,128)})) conditional(s32[]{:T(128)} %convert_element_type.52, (f32[1024,2,128]{2,0,1:T(8,128)S(1)}, f32[1024,128]{1,0:T(8,128)S(1)}, f32[1024,128]{1,0:T(8,128)}) %tuple.54, (s32[]{:T(128)}, bf16[1024,2,128]{2,0,1:T(8,128)(2,1)S(1)}, ...), branch_computations={%region_1.0_spmd, %region_2.2_spmd} | conditional | flops 2707947520 | bytes 48029768 | solution.py:39
  452.4 13.4 %conditional.4 = ((f32[1024,2,128]{2,0,1:T(8,128)S(1)}, f32[1024,128]{1,0:T(8,128)S(1)}, f32[1024,128]{1,0:T(8,128)})) conditional(s32[]{:T(128)} %convert_element_type.52, (f32[1024,2,128]{2,0,1:T(8,128)S(1)}, f32[1024,128]{1,0:T(8,128)S(1)}, f32[1024,128]{1,0:T(8,128)}) %tuple.54, (s32[]{:T(128)}, bf16[1024,2,128]{2,0,1:T(8,128)(2,1)S(1)}, ...), branch_computations={%region_1.0_spmd, %region_2.2_spmd} | conditional | flops 2707947520 | bytes 48029768 | solution.py:39
  486.5 13.4 %conditional.4 = ((f32[1024,2,128]{2,0,1:T(8,128)S(1)}, f32[1024,128]{1,0:T(8,128)S(1)}, f32[1024,128]{1,0:T(8,128)})) conditional(s32[]{:T(128)} %convert_element_type.52, (f32[1024,2,128]{2,0,1:T(8,128)S(1)}, f32[1024,128]{1,0:T(8,128)S(1)}, f32[1024,128]{1,0:T(8,128)}) %tuple.54, (s32[]{:T(128)}, bf16[1024,2,128]{2,0,1:T(8,128)(2,1)S(1)}, ...), branch_computations={%region_1.0_spmd, %region_2.2_spmd} | conditional | flops 2707947520 | bytes 48029768 | solution.py:39
  520.5 13.4 %conditional.4 = ((f32[1024,2,128]{2,0,1:T(8,128)S(1)}, f32[1024,128]{1,0:T(8,128)S(1)}, f32[1024,128]{1,0:T(8,128)})) conditional(s32[]{:T(128)} %convert_element_type.52, (f32[1024,2,128]{2,0,1:T(8,128)S(1)}, f32[1024,128]{1,0:T(8,128)S(1)}, f32[1024,128]{1,0:T(8,128)}) %tuple.54, (s32[]{:T(128)}, bf16[1024,2,128]{2,0,1:T(8,128)(2,1)S(1)}, ...), branch_computations={%region_1.0_spmd, %region_2.2_spmd} | conditional | flops 2707947520 | bytes 48029768 | solution.py:39
  554.6 13.4 %conditional.4 = ((f32[1024,2,128]{2,0,1:T(8,128)S(1)}, f32[1024,128]{1,0:T(8,128)S(1)}, f32[1024,128]{1,0:T(8,128)})) conditional(s32[]{:T(128)} %convert_element_type.52, (f32[1024,2,128]{2,0,1:T(8,128)S(1)}, f32[1024,128]{1,0:T(8,128)S(1)}, f32[1024,128]{1,0:T(8,128)}) %tuple.54, (s32[]{:T(128)}, bf16[1024,2,128]{2,0,1:T(8,128)(2,1)S(1)}, ...), branch_computations={%region_1.0_spmd, %region_2.2_spmd} | conditional | flops 2707947520 | bytes 48029768 | solution.py:39
  588.6 13.4 %conditional.4 = ((f32[1024,2,128]{2,0,1:T(8,128)S(1)}, f32[1024,128]{1,0:T(8,128)S(1)}, f32[1024,128]{1,0:T(8,128)})) conditional(s32[]{:T(128)} %convert_element_type.52, (f32[1024,2,128]{2,0,1:T(8,128)S(1)}, f32[1024,128]{1,0:T(8,128)S(1)}, f32[1024,128]{1,0:T(8,128)}) %tuple.54, (s32[]{:T(128)}, bf16[1024,2,128]{2,0,1:T(8,128)(2,1)S(1)}, ...), branch_computations={%region_1.0_spmd, %region_2.2_spmd} | conditional | flops 2707947520 | bytes 48029768 | solution.py:39
  622.7 13.4 %conditional.4 = ((f32[1024,2,128]{2,0,1:T(8,128)S(1)}, f32[1024,128]{1,0:T(8,128)S(1)}, f32[1024,128]{1,0:T(8,128)})) conditional(s32[]{:T(128)} %convert_element_type.52, (f32[1024,2,128]{2,0,1:T(8,128)S(1)}, f32[1024,128]{1,0:T(8,128)S(1)}, f32[1024,128]{1,0:T(8,128)}) %tuple.54, (s32[]{:T(128)}, bf16[1024,2,128]{2,0,1:T(8,128)(2,1)S(1)}, ...), branch_computations={%region_1.0_spmd, %region_2.2_spmd} | conditional | flops 2707947520 | bytes 48029768 | solution.py:39
  656.7 13.4 %conditional.4 = ((f32[1024,2,128]{2,0,1:T(8,128)S(1)}, f32[1024,128]{1,0:T(8,128)S(1)}, f32[1024,128]{1,0:T(8,128)})) conditional(s32[]{:T(128)} %convert_element_type.52, (f32[1024,2,128]{2,0,1:T(8,128)S(1)}, f32[1024,128]{1,0:T(8,128)S(1)}, f32[1024,128]{1,0:T(8,128)}) %tuple.54, (s32[]{:T(128)}, bf16[1024,2,128]{2,0,1:T(8,128)(2,1)S(1)}, ...), branch_computations={%region_1.0_spmd, %region_2.2_spmd} | conditional | flops 2707947520 | bytes 48029768 | solution.py:39
  690.8 13.4 %conditional.4 = ((f32[1024,2,128]{2,0,1:T(8,128)S(1)}, f32[1024,128]{1,0:T(8,128)S(1)}, f32[1024,128]{1,0:T(8,128)})) conditional(s32[]{:T(128)} %convert_element_type.52, (f32[1024,2,128]{2,0,1:T(8,128)S(1)}, f32[1024,128]{1,0:T(8,128)S(1)}, f32[1024,128]{1,0:T(8,128)}) %tuple.54, (s32[]{:T(128)}, bf16[1024,2,128]{2,0,1:T(8,128)(2,1)S(1)}, ...), branch_computations={%region_1.0_spmd, %region_2.2_spmd} | conditional | flops 2707947520 | bytes 48029768 | solution.py:39
  724.8 13.4 %conditional.4 = ((f32[1024,2,128]{2,0,1:T(8,128)S(1)}, f32[1024,128]{1,0:T(8,128)S(1)}, f32[1024,128]{1,0:T(8,128)})) conditional(s32[]{:T(128)} %convert_element_type.52, (f32[1024,2,128]{2,0,1:T(8,128)S(1)}, f32[1024,128]{1,0:T(8,128)S(1)}, f32[1024,128]{1,0:T(8,128)}) %tuple.54, (s32[]{:T(128)}, bf16[1024,2,128]{2,0,1:T(8,128)(2,1)S(1)}, ...), branch_computations={%region_1.0_spmd, %region_2.2_spmd} | conditional | flops 2707947520 | bytes 48029768 | solution.py:39
  758.8 13.4 %conditional.4 = ((f32[1024,2,128]{2,0,1:T(8,128)S(1)}, f32[1024,128]{1,0:T(8,128)S(1)}, f32[1024,128]{1,0:T(8,128)})) conditional(s32[]{:T(128)} %convert_element_type.52, (f32[1024,2,128]{2,0,1:T(8,128)S(1)}, f32[1024,128]{1,0:T(8,128)S(1)}, f32[1024,128]{1,0:T(8,128)}) %tuple.54, (s32[]{:T(128)}, bf16[1024,2,128]{2,0,1:T(8,128)(2,1)S(1)}, ...), branch_computations={%region_1.0_spmd, %region_2.2_spmd} | conditional | flops 2707947520 | bytes 48029768 | solution.py:39
  792.9 13.4 %conditional.4 = ((f32[1024,2,128]{2,0,1:T(8,128)S(1)}, f32[1024,128]{1,0:T(8,128)S(1)}, f32[1024,128]{1,0:T(8,128)})) conditional(s32[]{:T(128)} %convert_element_type.52, (f32[1024,2,128]{2,0,1:T(8,128)S(1)}, f32[1024,128]{1,0:T(8,128)S(1)}, f32[1024,128]{1,0:T(8,128)}) %tuple.54, (s32[]{:T(128)}, bf16[1024,2,128]{2,0,1:T(8,128)(2,1)S(1)}, ...), branch_computations={%region_1.0_spmd, %region_2.2_spmd} | conditional | flops 2707947520 | bytes 48029768 | solution.py:39
  826.9 13.4 %conditional.4 = ((f32[1024,2,128]{2,0,1:T(8,128)S(1)}, f32[1024,128]{1,0:T(8,128)S(1)}, f32[1024,128]{1,0:T(8,128)})) conditional(s32[]{:T(128)} %convert_element_type.52, (f32[1024,2,128]{2,0,1:T(8,128)S(1)}, f32[1024,128]{1,0:T(8,128)S(1)}, f32[1024,128]{1,0:T(8,128)}) %tuple.54, (s32[]{:T(128)}, bf16[1024,2,128]{2,0,1:T(8,128)(2,1)S(1)}, ...), branch_computations={%region_1.0_spmd, %region_2.2_spmd} | conditional | flops 2707947520 | bytes 48029768 | solution.py:39
  861.0 13.4 %conditional.4 = ((f32[1024,2,128]{2,0,1:T(8,128)S(1)}, f32[1024,128]{1,0:T(8,128)S(1)}, f32[1024,128]{1,0:T(8,128)})) conditional(s32[]{:T(128)} %convert_element_type.52, (f32[1024,2,128]{2,0,1:T(8,128)S(1)}, f32[1024,128]{1,0:T(8,128)S(1)}, f32[1024,128]{1,0:T(8,128)}) %tuple.54, (s32[]{:T(128)}, bf16[1024,2,128]{2,0,1:T(8,128)(2,1)S(1)}, ...), branch_computations={%region_1.0_spmd, %region_2.2_spmd} | conditional | flops 2707947520 | bytes 48029768 | solution.py:39
  895.0 13.4 %conditional.4 = ((f32[1024,2,128]{2,0,1:T(8,128)S(1)}, f32[1024,128]{1,0:T(8,128)S(1)}, f32[1024,128]{1,0:T(8,128)})) conditional(s32[]{:T(128)} %convert_element_type.52, (f32[1024,2,128]{2,0,1:T(8,128)S(1)}, f32[1024,128]{1,0:T(8,128)S(1)}, f32[1024,128]{1,0:T(8,128)}) %tuple.54, (s32[]{:T(128)}, bf16[1024,2,128]{2,0,1:T(8,128)(2,1)S(1)}, ...), branch_computations={%region_1.0_spmd, %region_2.2_spmd} | conditional | flops 2707947520 | bytes 48029768 | solution.py:39
  929.1 13.4 %conditional.4 = ((f32[1024,2,128]{2,0,1:T(8,128)S(1)}, f32[1024,128]{1,0:T(8,128)S(1)}, f32[1024,128]{1,0:T(8,128)})) conditional(s32[]{:T(128)} %convert_element_type.52, (f32[1024,2,128]{2,0,1:T(8,128)S(1)}, f32[1024,128]{1,0:T(8,128)S(1)}, f32[1024,128]{1,0:T(8,128)}) %tuple.54, (s32[]{:T(128)}, bf16[1024,2,128]{2,0,1:T(8,128)(2,1)S(1)}, ...), branch_computations={%region_1.0_spmd, %region_2.2_spmd} | conditional | flops 2707947520 | bytes 48029768 | solution.py:39
  963.1 13.4 %conditional.4 = ((f32[1024,2,128]{2,0,1:T(8,128)S(1)}, f32[1024,128]{1,0:T(8,128)S(1)}, f32[1024,128]{1,0:T(8,128)})) conditional(s32[]{:T(128)} %convert_element_type.52, (f32[1024,2,128]{2,0,1:T(8,128)S(1)}, f32[1024,128]{1,0:T(8,128)S(1)}, f32[1024,128]{1,0:T(8,128)}) %tuple.54, (s32[]{:T(128)}, bf16[1024,2,128]{2,0,1:T(8,128)(2,1)S(1)}, ...), branch_computations={%region_1.0_spmd, %region_2.2_spmd} | conditional | flops 2707947520 | bytes 48029768 | solution.py:39
  997.2 13.4 %conditional.4 = ((f32[1024,2,128]{2,0,1:T(8,128)S(1)}, f32[1024,128]{1,0:T(8,128)S(1)}, f32[1024,128]{1,0:T(8,128)})) conditional(s32[]{:T(128)} %convert_element_type.52, (f32[1024,2,128]{2,0,1:T(8,128)S(1)}, f32[1024,128]{1,0:T(8,128)S(1)}, f32[1024,128]{1,0:T(8,128)}) %tuple.54, (s32[]{:T(128)}, bf16[1024,2,128]{2,0,1:T(8,128)(2,1)S(1)}, ...), branch_computations={%region_1.0_spmd, %region_2.2_spmd} | conditional | flops 2707947520 | bytes 48029768 | solution.py:39
  1031.2 13.4 %conditional.4 = ((f32[1024,2,128]{2,0,1:T(8,128)S(1)}, f32[1024,128]{1,0:T(8,128)S(1)}, f32[1024,128]{1,0:T(8,128)})) conditional(s32[]{:T(128)} %convert_element_type.52, (f32[1024,2,128]{2,0,1:T(8,128)S(1)}, f32[1024,128]{1,0:T(8,128)S(1)}, f32[1024,128]{1,0:T(8,128)}) %tuple.54, (s32[]{:T(128)}, bf16[1024,2,128]{2,0,1:T(8,128)(2,1)S(1)}, ...), branch_computations={%region_1.0_spmd, %region_2.2_spmd} | conditional | flops 2707947520 | bytes 48029768 | solution.py:39
  (639 shorter events, 1074.9 us)
Async XLA Ops:
  23.5 16.9 %collective-permute-start = (bf16[1024,128]{1,0:T(8,128)(2,1)S(1)}, bf16[1024,128]{1,0:T(8,128)(2,1)S(1)}, u32[]{:S(2)}, u32[]{:S(2)}) collective-permute-start(bf16[1024,128]{1,0:T(8,128)(2,1)S(1)} %copy.52), channel_id=1, source_target_pairs={{0,1},{1,2},{2,3},{3,4},{4,5},{5,6},{6,7},{7,8},{8,9},{9,10},{10,1... | collective-permute-start | bytes 786440 | tf_op jit(solution)/shard_map/while/body/eval_jaxpr/ppermute | solution.py:43
  23.6 19.6 %collective-permute-start.1 = (bf16[1024,128]{1,0:T(8,128)(2,1)}, bf16[1024,128]{1,0:T(8,128)(2,1)S(1)}, u32[]{:S(2)}, u32[]{:S(2)}) collective-permute-start(bf16[1024,128]{1,0:T(8,128)(2,1)} %copy.53), channel_id=1, source_target_pairs={{0,1},{1,2},{2,3},{3,4},{4,5},{5,6},{6,7},{7,8},{8,9},{9,10},{10,1... | collective-permute-start | bytes 786440 | tf_op jit(solution)/shard_map/while/body/eval_jaxpr/ppermute | solution.py:44
  57.6 19.6 %collective-permute-start.1 = (bf16[1024,128]{1,0:T(8,128)(2,1)}, bf16[1024,128]{1,0:T(8,128)(2,1)S(1)}, u32[]{:S(2)}, u32[]{:S(2)}) collective-permute-start(bf16[1024,128]{1,0:T(8,128)(2,1)} %copy.53), channel_id=1, source_target_pairs={{0,1},{1,2},{2,3},{3,4},{4,5},{5,6},{6,7},{7,8},{8,9},{9,10},{10,1... | collective-permute-start | bytes 786440 | tf_op jit(solution)/shard_map/while/body/eval_jaxpr/ppermute | solution.py:44
  91.7 19.6 %collective-permute-start.1 = (bf16[1024,128]{1,0:T(8,128)(2,1)}, bf16[1024,128]{1,0:T(8,128)(2,1)S(1)}, u32[]{:S(2)}, u32[]{:S(2)}) collective-permute-start(bf16[1024,128]{1,0:T(8,128)(2,1)} %copy.53), channel_id=1, source_target_pairs={{0,1},{1,2},{2,3},{3,4},{4,5},{5,6},{6,7},{7,8},{8,9},{9,10},{10,1... | collective-permute-start | bytes 786440 | tf_op jit(solution)/shard_map/while/body/eval_jaxpr/ppermute | solution.py:44
  125.7 19.6 %collective-permute-start.1 = (bf16[1024,128]{1,0:T(8,128)(2,1)}, bf16[1024,128]{1,0:T(8,128)(2,1)S(1)}, u32[]{:S(2)}, u32[]{:S(2)}) collective-permute-start(bf16[1024,128]{1,0:T(8,128)(2,1)} %copy.53), channel_id=1, source_target_pairs={{0,1},{1,2},{2,3},{3,4},{4,5},{5,6},{6,7},{7,8},{8,9},{9,10},{10,1... | collective-permute-start | bytes 786440 | tf_op jit(solution)/shard_map/while/body/eval_jaxpr/ppermute | solution.py:44
  159.8 19.6 %collective-permute-start.1 = (bf16[1024,128]{1,0:T(8,128)(2,1)}, bf16[1024,128]{1,0:T(8,128)(2,1)S(1)}, u32[]{:S(2)}, u32[]{:S(2)}) collective-permute-start(bf16[1024,128]{1,0:T(8,128)(2,1)} %copy.53), channel_id=1, source_target_pairs={{0,1},{1,2},{2,3},{3,4},{4,5},{5,6},{6,7},{7,8},{8,9},{9,10},{10,1... | collective-permute-start | bytes 786440 | tf_op jit(solution)/shard_map/while/body/eval_jaxpr/ppermute | solution.py:44
  193.8 19.6 %collective-permute-start.1 = (bf16[1024,128]{1,0:T(8,128)(2,1)}, bf16[1024,128]{1,0:T(8,128)(2,1)S(1)}, u32[]{:S(2)}, u32[]{:S(2)}) collective-permute-start(bf16[1024,128]{1,0:T(8,128)(2,1)} %copy.53), channel_id=1, source_target_pairs={{0,1},{1,2},{2,3},{3,4},{4,5},{5,6},{6,7},{7,8},{8,9},{9,10},{10,1... | collective-permute-start | bytes 786440 | tf_op jit(solution)/shard_map/while/body/eval_jaxpr/ppermute | solution.py:44
  227.8 19.6 %collective-permute-start.1 = (bf16[1024,128]{1,0:T(8,128)(2,1)}, bf16[1024,128]{1,0:T(8,128)(2,1)S(1)}, u32[]{:S(2)}, u32[]{:S(2)}) collective-permute-start(bf16[1024,128]{1,0:T(8,128)(2,1)} %copy.53), channel_id=1, source_target_pairs={{0,1},{1,2},{2,3},{3,4},{4,5},{5,6},{6,7},{7,8},{8,9},{9,10},{10,1... | collective-permute-start | bytes 786440 | tf_op jit(solution)/shard_map/while/body/eval_jaxpr/ppermute | solution.py:44
  261.9 19.6 %collective-permute-start.1 = (bf16[1024,128]{1,0:T(8,128)(2,1)}, bf16[1024,128]{1,0:T(8,128)(2,1)S(1)}, u32[]{:S(2)}, u32[]{:S(2)}) collective-permute-start(bf16[1024,128]{1,0:T(8,128)(2,1)} %copy.53), channel_id=1, source_target_pairs={{0,1},{1,2},{2,3},{3,4},{4,5},{5,6},{6,7},{7,8},{8,9},{9,10},{10,1... | collective-permute-start | bytes 786440 | tf_op jit(solution)/shard_map/while/body/eval_jaxpr/ppermute | solution.py:44
  295.9 19.6 %collective-permute-start.1 = (bf16[1024,128]{1,0:T(8,128)(2,1)}, bf16[1024,128]{1,0:T(8,128)(2,1)S(1)}, u32[]{:S(2)}, u32[]{:S(2)}) collective-permute-start(bf16[1024,128]{1,0:T(8,128)(2,1)} %copy.53), channel_id=1, source_target_pairs={{0,1},{1,2},{2,3},{3,4},{4,5},{5,6},{6,7},{7,8},{8,9},{9,10},{10,1... | collective-permute-start | bytes 786440 | tf_op jit(solution)/shard_map/while/body/eval_jaxpr/ppermute | solution.py:44
  330.0 19.6 %collective-permute-start.1 = (bf16[1024,128]{1,0:T(8,128)(2,1)}, bf16[1024,128]{1,0:T(8,128)(2,1)S(1)}, u32[]{:S(2)}, u32[]{:S(2)}) collective-permute-start(bf16[1024,128]{1,0:T(8,128)(2,1)} %copy.53), channel_id=1, source_target_pairs={{0,1},{1,2},{2,3},{3,4},{4,5},{5,6},{6,7},{7,8},{8,9},{9,10},{10,1... | collective-permute-start | bytes 786440 | tf_op jit(solution)/shard_map/while/body/eval_jaxpr/ppermute | solution.py:44
  364.0 19.6 %collective-permute-start.1 = (bf16[1024,128]{1,0:T(8,128)(2,1)}, bf16[1024,128]{1,0:T(8,128)(2,1)S(1)}, u32[]{:S(2)}, u32[]{:S(2)}) collective-permute-start(bf16[1024,128]{1,0:T(8,128)(2,1)} %copy.53), channel_id=1, source_target_pairs={{0,1},{1,2},{2,3},{3,4},{4,5},{5,6},{6,7},{7,8},{8,9},{9,10},{10,1... | collective-permute-start | bytes 786440 | tf_op jit(solution)/shard_map/while/body/eval_jaxpr/ppermute | solution.py:44
  398.1 19.6 %collective-permute-start.1 = (bf16[1024,128]{1,0:T(8,128)(2,1)}, bf16[1024,128]{1,0:T(8,128)(2,1)S(1)}, u32[]{:S(2)}, u32[]{:S(2)}) collective-permute-start(bf16[1024,128]{1,0:T(8,128)(2,1)} %copy.53), channel_id=1, source_target_pairs={{0,1},{1,2},{2,3},{3,4},{4,5},{5,6},{6,7},{7,8},{8,9},{9,10},{10,1... | collective-permute-start | bytes 786440 | tf_op jit(solution)/shard_map/while/body/eval_jaxpr/ppermute | solution.py:44
  432.1 19.6 %collective-permute-start.1 = (bf16[1024,128]{1,0:T(8,128)(2,1)}, bf16[1024,128]{1,0:T(8,128)(2,1)S(1)}, u32[]{:S(2)}, u32[]{:S(2)}) collective-permute-start(bf16[1024,128]{1,0:T(8,128)(2,1)} %copy.53), channel_id=1, source_target_pairs={{0,1},{1,2},{2,3},{3,4},{4,5},{5,6},{6,7},{7,8},{8,9},{9,10},{10,1... | collective-permute-start | bytes 786440 | tf_op jit(solution)/shard_map/while/body/eval_jaxpr/ppermute | solution.py:44
  466.2 19.6 %collective-permute-start.1 = (bf16[1024,128]{1,0:T(8,128)(2,1)}, bf16[1024,128]{1,0:T(8,128)(2,1)S(1)}, u32[]{:S(2)}, u32[]{:S(2)}) collective-permute-start(bf16[1024,128]{1,0:T(8,128)(2,1)} %copy.53), channel_id=1, source_target_pairs={{0,1},{1,2},{2,3},{3,4},{4,5},{5,6},{6,7},{7,8},{8,9},{9,10},{10,1... | collective-permute-start | bytes 786440 | tf_op jit(solution)/shard_map/while/body/eval_jaxpr/ppermute | solution.py:44
  500.2 19.6 %collective-permute-start.1 = (bf16[1024,128]{1,0:T(8,128)(2,1)}, bf16[1024,128]{1,0:T(8,128)(2,1)S(1)}, u32[]{:S(2)}, u32[]{:S(2)}) collective-permute-start(bf16[1024,128]{1,0:T(8,128)(2,1)} %copy.53), channel_id=1, source_target_pairs={{0,1},{1,2},{2,3},{3,4},{4,5},{5,6},{6,7},{7,8},{8,9},{9,10},{10,1... | collective-permute-start | bytes 786440 | tf_op jit(solution)/shard_map/while/body/eval_jaxpr/ppermute | solution.py:44
  534.3 19.6 %collective-permute-start.1 = (bf16[1024,128]{1,0:T(8,128)(2,1)}, bf16[1024,128]{1,0:T(8,128)(2,1)S(1)}, u32[]{:S(2)}, u32[]{:S(2)}) collective-permute-start(bf16[1024,128]{1,0:T(8,128)(2,1)} %copy.53), channel_id=1, source_target_pairs={{0,1},{1,2},{2,3},{3,4},{4,5},{5,6},{6,7},{7,8},{8,9},{9,10},{10,1... | collective-permute-start | bytes 786440 | tf_op jit(solution)/shard_map/while/body/eval_jaxpr/ppermute | solution.py:44
  568.3 19.6 %collective-permute-start.1 = (bf16[1024,128]{1,0:T(8,128)(2,1)}, bf16[1024,128]{1,0:T(8,128)(2,1)S(1)}, u32[]{:S(2)}, u32[]{:S(2)}) collective-permute-start(bf16[1024,128]{1,0:T(8,128)(2,1)} %copy.53), channel_id=1, source_target_pairs={{0,1},{1,2},{2,3},{3,4},{4,5},{5,6},{6,7},{7,8},{8,9},{9,10},{10,1... | collective-permute-start | bytes 786440 | tf_op jit(solution)/shard_map/while/body/eval_jaxpr/ppermute | solution.py:44
  602.4 19.6 %collective-permute-start.1 = (bf16[1024,128]{1,0:T(8,128)(2,1)}, bf16[1024,128]{1,0:T(8,128)(2,1)S(1)}, u32[]{:S(2)}, u32[]{:S(2)}) collective-permute-start(bf16[1024,128]{1,0:T(8,128)(2,1)} %copy.53), channel_id=1, source_target_pairs={{0,1},{1,2},{2,3},{3,4},{4,5},{5,6},{6,7},{7,8},{8,9},{9,10},{10,1... | collective-permute-start | bytes 786440 | tf_op jit(solution)/shard_map/while/body/eval_jaxpr/ppermute | solution.py:44
  636.4 19.6 %collective-permute-start.1 = (bf16[1024,128]{1,0:T(8,128)(2,1)}, bf16[1024,128]{1,0:T(8,128)(2,1)S(1)}, u32[]{:S(2)}, u32[]{:S(2)}) collective-permute-start(bf16[1024,128]{1,0:T(8,128)(2,1)} %copy.53), channel_id=1, source_target_pairs={{0,1},{1,2},{2,3},{3,4},{4,5},{5,6},{6,7},{7,8},{8,9},{9,10},{10,1... | collective-permute-start | bytes 786440 | tf_op jit(solution)/shard_map/while/body/eval_jaxpr/ppermute | solution.py:44
  670.4 19.6 %collective-permute-start.1 = (bf16[1024,128]{1,0:T(8,128)(2,1)}, bf16[1024,128]{1,0:T(8,128)(2,1)S(1)}, u32[]{:S(2)}, u32[]{:S(2)}) collective-permute-start(bf16[1024,128]{1,0:T(8,128)(2,1)} %copy.53), channel_id=1, source_target_pairs={{0,1},{1,2},{2,3},{3,4},{4,5},{5,6},{6,7},{7,8},{8,9},{9,10},{10,1... | collective-permute-start | bytes 786440 | tf_op jit(solution)/shard_map/while/body/eval_jaxpr/ppermute | solution.py:44
  704.5 19.6 %collective-permute-start.1 = (bf16[1024,128]{1,0:T(8,128)(2,1)}, bf16[1024,128]{1,0:T(8,128)(2,1)S(1)}, u32[]{:S(2)}, u32[]{:S(2)}) collective-permute-start(bf16[1024,128]{1,0:T(8,128)(2,1)} %copy.53), channel_id=1, source_target_pairs={{0,1},{1,2},{2,3},{3,4},{4,5},{5,6},{6,7},{7,8},{8,9},{9,10},{10,1... | collective-permute-start | bytes 786440 | tf_op jit(solution)/shard_map/while/body/eval_jaxpr/ppermute | solution.py:44
  738.5 19.6 %collective-permute-start.1 = (bf16[1024,128]{1,0:T(8,128)(2,1)}, bf16[1024,128]{1,0:T(8,128)(2,1)S(1)}, u32[]{:S(2)}, u32[]{:S(2)}) collective-permute-start(bf16[1024,128]{1,0:T(8,128)(2,1)} %copy.53), channel_id=1, source_target_pairs={{0,1},{1,2},{2,3},{3,4},{4,5},{5,6},{6,7},{7,8},{8,9},{9,10},{10,1... | collective-permute-start | bytes 786440 | tf_op jit(solution)/shard_map/while/body/eval_jaxpr/ppermute | solution.py:44
  772.6 19.6 %collective-permute-start.1 = (bf16[1024,128]{1,0:T(8,128)(2,1)}, bf16[1024,128]{1,0:T(8,128)(2,1)S(1)}, u32[]{:S(2)}, u32[]{:S(2)}) collective-permute-start(bf16[1024,128]{1,0:T(8,128)(2,1)} %copy.53), channel_id=1, source_target_pairs={{0,1},{1,2},{2,3},{3,4},{4,5},{5,6},{6,7},{7,8},{8,9},{9,10},{10,1... | collective-permute-start | bytes 786440 | tf_op jit(solution)/shard_map/while/body/eval_jaxpr/ppermute | solution.py:44
  806.6 19.6 %collective-permute-start.1 = (bf16[1024,128]{1,0:T(8,128)(2,1)}, bf16[1024,128]{1,0:T(8,128)(2,1)S(1)}, u32[]{:S(2)}, u32[]{:S(2)}) collective-permute-start(bf16[1024,128]{1,0:T(8,128)(2,1)} %copy.53), channel_id=1, source_target_pairs={{0,1},{1,2},{2,3},{3,4},{4,5},{5,6},{6,7},{7,8},{8,9},{9,10},{10,1... | collective-permute-start | bytes 786440 | tf_op jit(solution)/shard_map/while/body/eval_jaxpr/ppermute | solution.py:44
  840.7 19.6 %collective-permute-start.1 = (bf16[1024,128]{1,0:T(8,128)(2,1)}, bf16[1024,128]{1,0:T(8,128)(2,1)S(1)}, u32[]{:S(2)}, u32[]{:S(2)}) collective-permute-start(bf16[1024,128]{1,0:T(8,128)(2,1)} %copy.53), channel_id=1, source_target_pairs={{0,1},{1,2},{2,3},{3,4},{4,5},{5,6},{6,7},{7,8},{8,9},{9,10},{10,1... | collective-permute-start | bytes 786440 | tf_op jit(solution)/shard_map/while/body/eval_jaxpr/ppermute | solution.py:44
  874.7 19.6 %collective-permute-start.1 = (bf16[1024,128]{1,0:T(8,128)(2,1)}, bf16[1024,128]{1,0:T(8,128)(2,1)S(1)}, u32[]{:S(2)}, u32[]{:S(2)}) collective-permute-start(bf16[1024,128]{1,0:T(8,128)(2,1)} %copy.53), channel_id=1, source_target_pairs={{0,1},{1,2},{2,3},{3,4},{4,5},{5,6},{6,7},{7,8},{8,9},{9,10},{10,1... | collective-permute-start | bytes 786440 | tf_op jit(solution)/shard_map/while/body/eval_jaxpr/ppermute | solution.py:44
  908.8 19.6 %collective-permute-start.1 = (bf16[1024,128]{1,0:T(8,128)(2,1)}, bf16[1024,128]{1,0:T(8,128)(2,1)S(1)}, u32[]{:S(2)}, u32[]{:S(2)}) collective-permute-start(bf16[1024,128]{1,0:T(8,128)(2,1)} %copy.53), channel_id=1, source_target_pairs={{0,1},{1,2},{2,3},{3,4},{4,5},{5,6},{6,7},{7,8},{8,9},{9,10},{10,1... | collective-permute-start | bytes 786440 | tf_op jit(solution)/shard_map/while/body/eval_jaxpr/ppermute | solution.py:44
  942.8 19.6 %collective-permute-start.1 = (bf16[1024,128]{1,0:T(8,128)(2,1)}, bf16[1024,128]{1,0:T(8,128)(2,1)S(1)}, u32[]{:S(2)}, u32[]{:S(2)}) collective-permute-start(bf16[1024,128]{1,0:T(8,128)(2,1)} %copy.53), channel_id=1, source_target_pairs={{0,1},{1,2},{2,3},{3,4},{4,5},{5,6},{6,7},{7,8},{8,9},{9,10},{10,1... | collective-permute-start | bytes 786440 | tf_op jit(solution)/shard_map/while/body/eval_jaxpr/ppermute | solution.py:44
  976.9 19.6 %collective-permute-start.1 = (bf16[1024,128]{1,0:T(8,128)(2,1)}, bf16[1024,128]{1,0:T(8,128)(2,1)S(1)}, u32[]{:S(2)}, u32[]{:S(2)}) collective-permute-start(bf16[1024,128]{1,0:T(8,128)(2,1)} %copy.53), channel_id=1, source_target_pairs={{0,1},{1,2},{2,3},{3,4},{4,5},{5,6},{6,7},{7,8},{8,9},{9,10},{10,1... | collective-permute-start | bytes 786440 | tf_op jit(solution)/shard_map/while/body/eval_jaxpr/ppermute | solution.py:44
  1010.9 19.6 %collective-permute-start.1 = (bf16[1024,128]{1,0:T(8,128)(2,1)}, bf16[1024,128]{1,0:T(8,128)(2,1)S(1)}, u32[]{:S(2)}, u32[]{:S(2)}) collective-permute-start(bf16[1024,128]{1,0:T(8,128)(2,1)} %copy.53), channel_id=1, source_target_pairs={{0,1},{1,2},{2,3},{3,4},{4,5},{5,6},{6,7},{7,8},{8,9},{9,10},{10,1... | collective-permute-start | bytes 786440 | tf_op jit(solution)/shard_map/while/body/eval_jaxpr/ppermute | solution.py:44
  1045.0 19.6 %collective-permute-start.1 = (bf16[1024,128]{1,0:T(8,128)(2,1)}, bf16[1024,128]{1,0:T(8,128)(2,1)S(1)}, u32[]{:S(2)}, u32[]{:S(2)}) collective-permute-start(bf16[1024,128]{1,0:T(8,128)(2,1)} %copy.53), channel_id=1, source_target_pairs={{0,1},{1,2},{2,3},{3,4},{4,5},{5,6},{6,7},{7,8},{8,9},{9,10},{10,1... | collective-permute-start | bytes 786440 | tf_op jit(solution)/shard_map/while/body/eval_jaxpr/ppermute | solution.py:44
  (125 other events, 1288.3 us)
where the time goes:
time: 1080 us
  waiting for transfers between devices  555 us (51%)
  matrix products  402 us (37%)
  local copies, waits for them, and re-layouts  87 us (8%)
  other arithmetic  15.8 us (1%)
  starting transfers between devices  13.5 us (1%)
    ppermute x31, waiting for transfers between devices, step_fn(): dk_next = lax.ppermute(dk_acc, 'cp', forward_perm)  255 us
    dot_general x31, matrix products, pair_update(): jnp.einsum('rgc,rgd->cd', prob_low, d_out, preferred_element_type=jnp.flo...  150 us
    ppermute x31, waiting for transfers between devices, step_fn(): dv_next = lax.ppermute(dv_acc, 'cp', forward_perm)  142 us
    dot_general x31, matrix products, pair_scores(): jnp.einsum('rgd,cd->rgc', do_block, v_block, preferred_element_type=jnp.f...  130 us
    ppermute x31, waiting for transfers between devices, step_fn(): v_next = lax.ppermute(v_cur, 'cp', forward_perm)  87.1 us
    ppermute x31, waiting for transfers between devices, step_fn(): k_next = lax.ppermute(k_cur, 'cp', forward_perm)  62.5 us
    while x62, local copies, waits for them, and re-layouts  56.9 us
    dot_general x31, matrix products, pair_update(): jnp.einsum('rgc,rgd->cd', score_low, q_tok, preferred_element_type=jnp.fl...  42.1 us
  transfers between devices with their start and end apart: 126, of which 125 were waited for; matrix products, arithmetic and copies ran while one was open for 5% of the time, Pallas kernels for 0%

commit v1 on v0

v1 whole, which is shorter than its diff:
```python
import functools
import math

import jax
import jax.numpy as jnp
from jax import lax
from jax.experimental import pallas as pl
from jax.experimental.pallas import tpu as pltpu
from jax.sharding import PartitionSpec as P

MESH = pl.DeviceIdType.MESH
NT = (((1,), (1,)), ((), ()))
BF16, F32 = jnp.bfloat16, jnp.float32

ROWS = (
    [(q, dx, 0, 1) for q in (3, 2, 1) for dx in (1, 3, 2, 0)],
    [(2, 2, 1, 0), (2, 3, 1, 0), (3, 2, 1, 0), (3, 3, 1, 0)]
    + [(q, dx, 0, 1) for q in (3, 2) for dx in (1, 3, 2, 0)],
    [(2, 0, 1, 2), (2, 1, 1, 2), (3, 0, 1, 2), (3, 1, 1, 2)]
    + [(3, dx, 0, k) for dx in (1, 3, 2, 0) for k in (0, 1)],
    [(q, dx, 0, 2) for dx in (1, 3) for q in (3, 2, 1)]
    + [(q, dx, 0, 2) for q in (1, 2, 3) for dx in (2, 0)],
)
N_TASK = 12


def pack(rows, bits):
    return [sum(v << (bits * u) for u, v in enumerate(row)) for row in rows]


def last_use(row, key):
    return [int(all(key(e) != key(row[w]) for e in row[w + 1:])) for w in range(len(row))]


def first_use(row, key):
    return [int(all(key(e) != key(row[w]) for e in row[:w])) for w in range(len(row))]


T_Q = pack([[e[0] for e in r] for r in ROWS], 2)
T_X = pack([[e[1] for e in r] for r in ROWS], 2)
T_ABS = pack([[e[2] for e in r] for r in ROWS], 1)
T_KIND = pack([[e[3] for e in r] for r in ROWS], 2)
T_KVLAST = pack([last_use(r, lambda e: e[1:]) for r in ROWS], 1)
T_QLAST = pack([[f * int(e[0] != y) for f, e in zip(last_use(r, lambda e: e[0]), r)] for y, r in enumerate(ROWS)], 1)
T_QFIRST = pack([[f * int(e[0] != y) for f, e in zip(first_use(r, lambda e: e[0]), r)] for y, r in enumerate(ROWS)], 1)
T_TAKEN = pack([[f * int(e[3] == 2) for f, e in zip(first_use(r, lambda e: e[1:]), r)] for r in ROWS], 1)


def attn_grad_kernel(side, scale, q_hbm, do_hbm, st_hbm, k_hbm, v_hbm, gq_ref, gk_ref, gv_ref,
                     qb, dob, stb, qtb, dotb, kb, vb, dqa, dkv, dqr, par, ici, fin,
                     ld_sem, q_ss, q_rs, kv_s1, kv_s2, kv_s3, kv_s4, kv_rs,
                     par_ss, par_rs, ici_ss, ici_rs, dq_ss, dq_rs, fin_ss, fin_rs):
    rows2, head = qb.shape[1], qb.shape[2]
    tok = kb.shape[1]
    sub = tok // 4
    exp_scale = scale * math.log2(math.e)
    me = lax.axis_index('cp')
    c = lax.rem(me, 2)
    x = lax.rem(me // 2, side)
    y = me // (2 * side)
    partner = me + 1 - 2 * c
    own = 2 * x + c

    def dev(yy, xx, cc):
        return (yy * side + xx) * 2 + cc

    def wrap(v):
        return lax.rem(v, side)

    def copy(src, dst, ssem, rsem, device):
        return pltpu.make_async_remote_copy(src_ref=src, dst_ref=dst, send_sem=ssem, recv_sem=rsem,
                                            device_id={'cp': device}, device_id_type=MESH)

    def field(table, bits, u):
        word = jnp.where(y == 0, table[0], jnp.where(y == 1, table[1], jnp.where(y == 2, table[2], table[3])))
        return lax.rem(lax.shift_right_logical(word, bits * u), 1 << bits)

    def decode(u):
        kind = field(T_KIND, 2, u)
        xv = field(T_X, 2, u)
        xs = jnp.where(field(T_ABS, 1, u) == 1, xv, wrap(x + xv))
        taken = kind == 2
        slot = jnp.where(taken, 8 + xs, 2 * xs + kind)
        idx = jnp.where(taken, 4 + xs, xs)
        resp = jnp.where(taken, 0, kind)
        return slot, xs, idx, resp

    def feeds(src, dst):
        return jnp.logical_or(src < dst, jnp.logical_and(src == 3, jnp.logical_and(dst > 0, dst < 3)))

    def local_only(yy, xx, cc):
        low = jnp.logical_and(cc == 0, jnp.logical_or(yy == 0, jnp.logical_and(yy == 1, xx < 2)))
        return jnp.logical_or(yy == 3, low)

    gives = jnp.logical_and(c == 0, jnp.logical_or(y == 0, jnp.logical_and(y == 1, x < 2)))
    takes = jnp.logical_and(c == 0, jnp.logical_or(y == 3, jnp.logical_and(y == 2, x < 2)))
    mirror = dev(3 - y, x, c)

    loads = [pltpu.make_async_copy(src, dst, ld_sem.at[i]) for i, (src, dst) in enumerate((
        (k_hbm, kb.at[own]), (v_hbm, vb.at[own]), (q_hbm, qb.at[y]), (do_hbm, dob.at[y]), (st_hbm, stb.at[y])))]
    for load in loads:
        load.start()

    barrier = pltpu.get_barrier_semaphore()
    peers = [partner] + [dev(y, wrap(x + d), c) for d in (1, 2, 3)] + [dev(wrap(y + d), x, c) for d in (1, 2, 3)]
    for peer in peers:
        pl.semaphore_signal(barrier, inc=1, device_id={'cp': peer}, device_id_type=MESH)
    pl.semaphore_wait(barrier, len(peers))

    def kv_pair(slot, ssem, device):
        return (copy(kb.at[slot], kb.at[slot], ssem.at[0], kv_rs.at[slot, 0], device),
                copy(vb.at[slot], vb.at[slot], ssem.at[1], kv_rs.at[slot, 1], device))

    def start(pair):
        for p in pair:
            p.start()

    def kv_wait(slot):
        for p in kv_pair(slot, kv_s3, partner):
            p.wait_recv()

    def q_trio(row, dst_row):
        device = dev(dst_row, x, c)
        return tuple(copy(b.at[row], b.at[row], q_ss.at[dst_row, i], q_rs.at[row, i], device)
                     for i, b in enumerate((qb, dob, stb)))

    def par_copy(slot, idx):
        return copy(dkv.at[slot], par.at[idx], par_ss.at[idx], par_rs.at[idx], partner)

    def ici_copy(slot, xs, cls):
        return copy(dkv.at[slot], ici.at[4 * cls + x], ici_ss.at[4 * cls + xs], ici_rs.at[4 * cls + x], dev(y, xs, c))

    def ici_wait(cls, xs):
        copy(dkv.at[own], ici.at[4 * cls + xs], ici_ss.at[4 * cls + xs], ici_rs.at[4 * cls + xs], partner).wait_recv()

    def dq_copy(row):
        return copy(dqa.at[row], dqr.at[y], dq_ss.at[row], dq_rs.at[y], dev(row, x, c))

    def fin_copy():
        return copy(dkv.at[8 + x], fin, fin_ss, fin_rs, mirror)

    for load in loads[:2]:
        load.wait()
    start(kv_pair(own, kv_s1.at[0], partner))
    for d in (1, 3, 2):
        start(kv_pair(own, kv_s1.at[d], dev(y, wrap(x + d), c)))

    def give_copy():
        slot = 8 + x
        return (copy(kb.at[own], kb.at[slot], kv_s3.at[0], kv_rs.at[slot, 0], mirror),
                copy(vb.at[own], vb.at[slot], kv_s3.at[1], kv_rs.at[slot, 1], mirror))

    @pl.when(gives)
    def _():
        start(give_copy())

    for load in loads[2:]:
        load.wait()
    for d in (1, 3, 2):
        dst = wrap(y + d)

        @pl.when(feeds(dst, y))
        def _():
            start(q_trio(y, dst))

    def clear(ref, slots):
        def body(i, carry):
            ref[i] = jnp.zeros(ref.shape[1:], F32)
            return carry
        lax.fori_loop(0, slots, body, 0)

    clear(dkv, dkv.shape[0])
    clear(dqa, dqa.shape[0])

    def transpose_queries(row):
        for g in range(8):
            part = pl.ds(g * sub, sub)
            qtb[row, :, part] = qb[row, part, :].T
            dotb[row, :, part] = dob[row, part, :].T

    def piece(row, slot, start_row, width, u, masked):
        part = pl.ds(start_row, sub)
        k_t = kb[slot, :width, :]
        logits = lax.dot_general(qb[row, part, :], k_t, NT, preferred_element_type=F32)
        d_prob = lax.dot_general(dob[row, part, :], vb[slot, :width, :], NT, preferred_element_type=F32)
        stats = stb[row, :, part].T
        power = logits * exp_scale - stats[:, 0:1]
        if masked:
            r = lax.broadcasted_iota(jnp.int32, power.shape, 0) + u * sub
            power = jnp.where(lax.broadcasted_iota(jnp.int32, power.shape, 1) <= r, power, -1e30)
        prob = jnp.exp2(power)
        d_score = (prob * (d_prob - stats[:, 1:2])).astype(BF16)
        prob = prob.astype(BF16)
        dkv[slot, 1, :, :width] += jnp.dot(dotb[row, :, part], prob, preferred_element_type=F32)
        dkv[slot, 0, :, :width] += jnp.dot(qtb[row, :, part], d_score, preferred_element_type=F32)
        dqa[row, part, :] += jnp.dot(d_score, k_t, preferred_element_type=F32)

    def full_task(row, slot):
        def head_loop(g, carry):
            for u in range(4):
                piece(row, slot, pl.multiple_of(g * tok + u * sub, sub), tok, u, False)
            return carry
        lax.fori_loop(0, 2, head_loop, 0)

    def diag_task():
        def head_loop(g, carry):
            for u in range(4):
                piece(y, own, pl.multiple_of(g * tok + u * sub, sub), (u + 1) * sub, u, True)
            return carry
        lax.fori_loop(0, 2, head_loop, 0)

    def add_into(slot, other, oidx):
        def body(i, carry):
            part = pl.ds(pl.multiple_of(i * 32, 32), 32)
            for h in range(2):
                dkv[slot, h, part, :] += other[oidx, h, part, :]
            return carry
        lax.fori_loop(0, head // 32, body, 0)

    def reduce_chip(slot, xs, idx, cls):
        par_copy(slot, idx).wait_recv()
        add_into(slot, par, idx)

        @pl.when(xs != x)
        def _():
            ici_copy(slot, xs, cls).start()

    transpose_queries(y)
    diag_task()

    @pl.when(takes)
    def _():
        kv_wait(8 + x)
        start(kv_pair(8 + x, kv_s4.at[0], partner))
        for d in (1, 3, 2):
            start(kv_pair(8 + x, kv_s4.at[d], dev(y, wrap(x + d), c)))

    def after_diag(mine):
        for xs in range(4):
            cc = c if mine else 1 - c

            @pl.when(jnp.logical_and(local_only(y, xs, cc), xs <= x))
            def _():
                if mine:
                    reduce_chip(2 * xs + c, xs, xs, 0)
                else:
                    par_copy(2 * xs + 1 - c, xs).start()

    def step(t, carry):
        half = t // 2
        d = half + jnp.where(half == 2, 1, 0) - jnp.where(half == 3, 1, 0)
        x_d = wrap(x + d)
        mate = lax.rem(t, 2)
        c_d = jnp.where(mate == 0, c, 1 - c)
        u = jnp.maximum(t - 8, 0)
        first = t < 8
        slot_u, xs, idx, resp = decode(u)
        slot = jnp.where(first, 2 * x_d + c_d, slot_u)
        row = jnp.where(first, y, field(T_Q, 2, u))

        @pl.when(first)
        def _():
            kv_wait(slot)

            @pl.when(mate == 0)
            def _():
                start(kv_pair(slot, kv_s2.at[x_d], partner))

        later = jnp.logical_not(first)

        @pl.when(jnp.logical_and(later, field(T_QFIRST, 1, u) == 1))
        def _():
            for p in q_trio(row, row):
                p.wait_recv()
            transpose_queries(row)

        @pl.when(jnp.logical_and(later, field(T_TAKEN, 1, u) == 1))
        def _():
            @pl.when(jnp.logical_or(c == 1, xs != x))
            def _():
                kv_wait(slot)

            @pl.when(jnp.logical_and(c == 0, xs != x))
            def _():
                start(kv_pair(slot, kv_s2.at[4 + xs], partner))

        @pl.when(jnp.logical_or(later, 2 * x_d + c_d < own))
        def _():
            full_task(row, slot)

        @pl.when(t == 7)
        def _():
            after_diag(False)

        @pl.when(t == 9)
        def _():
            after_diag(True)

        @pl.when(jnp.logical_and(later, field(T_QLAST, 1, u) == 1))
        def _():
            dq_copy(row).start()

        done = field(T_KVLAST, 1, u) == 1

        @pl.when(jnp.logical_and(later, jnp.logical_and(done, c != resp)))
        def _():
            par_copy(slot, idx).start()

        before = jnp.maximum(u - 1, 0)
        slot_b, xs_b, idx_b, resp_b = decode(before)

        @pl.when(jnp.logical_and(u > 0, jnp.logical_and(field(T_KVLAST, 1, before) == 1, c == resp_b)))
        def _():
            reduce_chip(slot_b, xs_b, idx_b, idx_b // 4)
        return carry

    lax.fori_loop(1, 8 + N_TASK, step, 0)

    slot_b, xs_b, idx_b, resp_b = decode(jnp.int32(N_TASK - 1))

    @pl.when(c == resp_b)
    def _():
        reduce_chip(slot_b, xs_b, idx_b, idx_b // 4)

    @pl.when(takes)
    def _():
        for d in (1, 3, 2):
            ici_wait(1, wrap(x + d))
            add_into(8 + x, ici, 4 + wrap(x + d))
        fin_copy().start()

    for d in (1, 3, 2):
        xs = wrap(x + d)

        @pl.when(jnp.logical_or(jnp.logical_not(local_only(y, x, c)), xs > x))
        def _():
            ici_wait(0, xs)
            add_into(own, ici, xs)

    for d in (1, 3, 2):
        src = wrap(y + d)

        @pl.when(feeds(src, y))
        def _():
            copy(dqa.at[y], dqr.at[src], dq_ss.at[src], dq_rs.at[src], partner).wait_recv()

            def body(i, carry):
                part = pl.ds(pl.multiple_of(i * sub, sub), sub)
                dqa[y, part, :] += dqr[src, part, :]
                return carry
            lax.fori_loop(0, rows2 // sub, body, 0)

    @pl.when(gives)
    def _():
        fin_copy().wait_recv()

        def body(i, carry):
            part = pl.ds(pl.multiple_of(i * 32, 32), 32)
            for h in range(2):
                dkv[own, h, part, :] += fin[h, part, :]
            return carry
        lax.fori_loop(0, head // 32, body, 0)

    def out_q(i, carry):
        part = pl.ds(pl.multiple_of(i * sub, sub), sub)
        gq_ref[part, :] = (dqa[y, part, :] * scale).astype(BF16)
        return carry

    lax.fori_loop(0, rows2 // sub, out_q, 0)
    for g in range(4):
        part = pl.ds(g * sub, sub)
        gk_ref[part, :] = (dkv[own, 0, :, part] * scale).T.astype(BF16)
        gv_ref[part, :] = dkv[own, 1, :, part].T.astype(BF16)

    def sent(pair):
        for p in pair:
            p.wait_send()

    for d in range(4):
        sent(kv_pair(own, kv_s1.at[d], partner))
    for d in (1, 2, 3):
        sent(kv_pair(own, kv_s2.at[wrap(x + d)], partner))
        dst = wrap(y + d)

        @pl.when(feeds(dst, y))
        def _():
            sent(q_trio(y, dst))

        @pl.when(feeds(y, dst))
        def _():
            dq_copy(dst).wait_send()

    @pl.when(gives)
    def _():
        sent(give_copy())

    @pl.when(takes)
    def _():
        for d in range(4):
            sent(kv_pair(8 + x, kv_s4.at[d], partner))
        fin_copy().wait_send()

    for xs in range(4):
        has_taken = jnp.logical_or(y == 3, y == 2) if xs < 2 else y == 3

        @pl.when(jnp.logical_or(jnp.logical_not(local_only(y, xs, 1 - c)), xs <= x))
        def _():
            par_copy(2 * xs + 1 - c, xs).wait_send()

        @pl.when(jnp.logical_and(xs != x, jnp.logical_or(jnp.logical_not(local_only(y, xs, c)), xs < x)))
        def _():
            ici_copy(2 * xs + c, xs, 0).wait_send()

        @pl.when(jnp.logical_and(c == 1, has_taken))
        def _():
            par_copy(8 + xs, 4 + xs).wait_send()

        @pl.when(jnp.logical_and(jnp.logical_and(c == 0, xs != x), has_taken))
        def _():
            sent(kv_pair(8 + xs, kv_s2.at[4 + xs], partner))
            ici_copy(8 + xs, xs, 1).wait_send()


def solution(mesh):
    n_dev = mesh.shape['cp']
    side = math.isqrt(n_dev // 2)
    assert side * side * 2 == n_dev and side == len(ROWS)
    row_spec = P(('dp', 'cp'))

    def local_fn(q_tok, k_tok, v_tok, fwd_out, d_out, lse_row):
        tok, heads, head = q_tok.shape
        scale = head ** -0.5
        rows2 = tok * heads
        delta = jnp.sum(d_out.astype(F32) * fwd_out.astype(F32), axis=-1)
        stats = jnp.stack([lse_row * math.log2(math.e), delta]).transpose(0, 2, 1).reshape(2, rows2)
        stats = jnp.pad(stats, ((0, 6), (0, 0)))
        q_rows = q_tok.transpose(1, 0, 2).reshape(rows2, head)
        do_rows = d_out.transpose(1, 0, 2).reshape(rows2, head)
        hbm = pl.BlockSpec(memory_space=pl.ANY)
        vmem = pl.BlockSpec(memory_space=pltpu.VMEM)
        dma = pltpu.SemaphoreType.DMA
        gq, gk, gv = pl.pallas_call(
            functools.partial(attn_grad_kernel, side, scale),
            out_shape=[jax.ShapeDtypeStruct((rows2, head), BF16), jax.ShapeDtypeStruct((tok, head), BF16),
                       jax.ShapeDtypeStruct((tok, head), BF16)],
            in_specs=[hbm] * 5,
            out_specs=[vmem] * 3,
            scratch_shapes=[
                pltpu.VMEM((4, rows2, head), BF16), pltpu.VMEM((4, rows2, head), BF16), pltpu.VMEM((4, 8, rows2), F32),
                pltpu.VMEM((4, head, rows2), BF16), pltpu.VMEM((4, head, rows2), BF16),
                pltpu.VMEM((12, tok, head), BF16), pltpu.VMEM((12, tok, head), BF16),
                pltpu.VMEM((4, rows2, head), F32), pltpu.VMEM((12, 2, head, tok), F32), pltpu.VMEM((4, rows2, head), F32),
                pltpu.VMEM((8, 2, head, tok), F32), pltpu.VMEM((8, 2, head, tok), F32), pltpu.VMEM((2, head, tok), F32),
                dma((5,)), dma((4, 3)), dma((4, 3)), dma((4, 2)), dma((8, 2)), dma((2,)), dma((4, 2)), dma((12, 2)),
                dma((8,)), dma((8,)), dma((8,)), dma((8,)), dma((4,)), dma((4,)), dma, dma,
            ],
            compiler_params=pltpu.CompilerParams(collective_id=0, has_side_effects=True, vmem_limit_bytes=66 * 10 ** 6),
            name='attn_grad',
        )(q_rows, do_rows, stats, k_tok, v_tok)
        return gq.reshape(heads, tok, head).transpose(1, 0, 2), gk, gv

    return jax.shard_map(local_fn, mesh=mesh, in_specs=(row_spec,) * 6, out_specs=(row_spec,) * 3, check_vma=False)
```

time: 1080 us -> 168 us (0.16)
  the two profiles are of different devices: /device:TPU:126 before, /device:TPU:98 now
where the time goes in v1:
time: 168 us; the launch traced here: 167 us
  Pallas kernels  157 us (93%)
  local copies, waits for them, and re-layouts  7.86 us (5%)
  other arithmetic  1.96 us (1%)
    pallas_call x1, Pallas kernels, local_fn(): pl.pallas_call(functools.partial(attn_grad_kernel, side, scale), out_shap...  157 us

profile of v1, /device:TPU:98, one launch (start us, length us, event | category | flops | bytes accessed | tf_op | source)
XLA Modules:
  0.0 167.4 jit_solution(18335496774168324493)
XLA Ops:
  0.6 0.7 multiply_bitcast_fusion
  1.3 0.0 copy-start
  1.3 0.0 copy-start.1
  1.3 2.0 %copy.17 = bf16[2,1024,128]{2,1,0:T(8,128)(2,1)} copy(bf16[2,1024,128]{2,0,1:T(2,128)(2,1)} %bitcast.19) | data formatting | bytes 1048576 | tf_op jit(solution)/shard_map/transpose | solution.py:437
  3.3 0.0 copy-done
  3.3 0.0 copy-done.1
  3.3 1.2 multiply_reduce_fusion
  4.6 0.2 copy.19
  4.8 0.6 pad.4.st_hbm
  5.4 0.9 copy.18
  6.3 156.9 %attn_grad.1 = (bf16[2048,128]{1,0:T(8,128)(2,1)}, bf16[1024,128]{1,0:T(8,128)(2,1)}, bf16[1024,128]{1,0:T(8,128)(2,1)}) custom-call(bf16[2048,128]{1,0:T(8,128)(2,1)} %bitcast.16, bf16[2048,128]{1,0:T(8,128)(2,1)} %bitcast.17, f32[8,2048]{1,0:T(8,128)} %pad.4.st_hbm, bf16[1024,128]{1,0:T(8,128)(2,1)} %k_hbm.1, bf16[1024,128]{1,0:T(8,128)(2,1)} %v_hbm.1), custom_call_target="tpu_custom_call" | custom-call | tf_op jit(solution)/shard_map/attn_grad/pallas_call | solution.py:442
  163.2 0.0 copy-start.3
  163.2 2.4 %copy.23 = bf16[2,1024,128]{2,0,1:T(2,128)(2,1)} copy(bf16[2,1024,128]{2,1,0:T(8,128)(2,1)} %bitcast.21) | data formatting | bytes 1048576 | tf_op jit(solution)/shard_map/reshape | solution.py:460
  165.7 0.0 copy-done.3
  165.7 0.0 copy-start.2
  165.7 0.7 copy.26
  166.4 0.3 copy-done.2
  166.7 0.7 copy.27
  (2 shorter events, 0.0 us)
Async XLA Ops:
  1.3 2.0 %copy-start = (bf16[1024,2,128]{2,1,0:T(2,128)(2,1)S(1)}, bf16[1024,2,128]{2,1,0:T(2,128)(2,1)}, u32[]{:S(2)}) copy-start(bf16[1024,2,128]{2,1,0:T(2,128)(2,1)} %param.10) | copy-start | bytes 1572868
  1.3 2.0 %copy-start.1 = (bf16[1024,2,128]{2,1,0:T(2,128)(2,1)S(1)}, bf16[1024,2,128]{2,1,0:T(2,128)(2,1)}, u32[]{:S(2)}) copy-start(bf16[1024,2,128]{2,1,0:T(2,128)(2,1)} %param.9) | copy-start | bytes 1572868
  163.2 2.4 %copy-start.3 = (bf16[1024,128]{1,0:T(8,128)(2,1)S(1)}, bf16[1024,128]{1,0:T(8,128)(2,1)}, u32[]{:S(2)}) copy-start(bf16[1024,128]{1,0:T(8,128)(2,1)} %get-tuple-element.13) | copy-start | bytes 786436
  165.7 1.0 copy-start.2

commit v2 on v1

--- a/solution.py
+++ b/solution.py
@@ -13,13 +13,13 @@
 BF16, F32 = jnp.bfloat16, jnp.float32
 
 ROWS = (
-    [(q, dx, 0, 1) for q in (3, 2, 1) for dx in (1, 3, 2, 0)],
+    [(q, dx, 0, 1) for q in (3, 2, 1) for dx in (2, 1, 3, 0)],
     [(2, 2, 1, 0), (2, 3, 1, 0), (3, 2, 1, 0), (3, 3, 1, 0)]
-    + [(q, dx, 0, 1) for q in (3, 2) for dx in (1, 3, 2, 0)],
+    + [(q, dx, 0, 1) for q in (3, 2) for dx in (2, 1, 3, 0)],
     [(2, 0, 1, 2), (2, 1, 1, 2), (3, 0, 1, 2), (3, 1, 1, 2)]
-    + [(3, dx, 0, k) for dx in (1, 3, 2, 0) for k in (0, 1)],
-    [(q, dx, 0, 2) for dx in (1, 3) for q in (3, 2, 1)]
-    + [(q, dx, 0, 2) for q in (1, 2, 3) for dx in (2, 0)],
+    + [(3, dx, 0, k) for dx in (2, 1, 3, 0) for k in (0, 1)],
+    [(q, dx, 0, 2) for dx in (2, 1) for q in (3, 2, 1)]
+    + [(q, dx, 0, 2) for q in (1, 2, 3) for dx in (3, 0)],
 )
 N_TASK = 12
 
@@ -47,9 +47,9 @@
 
 
 def attn_grad_kernel(side, scale, q_hbm, do_hbm, st_hbm, k_hbm, v_hbm, gq_ref, gk_ref, gv_ref,
-                     qb, dob, stb, qtb, dotb, kb, vb, dqa, dkv, dqr, par, ici, fin,
-                     ld_sem, q_ss, q_rs, kv_s1, kv_s2, kv_s3, kv_s4, kv_rs,
-                     par_ss, par_rs, ici_ss, ici_rs, dq_ss, dq_rs, fin_ss, fin_rs):
+                     qb, dob, stb, qtb, dotb, kb, vb, dqa, dkv, dqr, par, ici, half, fin,
+                     ld_sem, q_ss, q_rs, kv_s1, kv_s2, kv_s3, kv_s4, kv_s5, kv_rs,
+                     par_ss, par_rs, ici_ss, ici_rs, half_ss, half_rs, dq_ss, dq_rs, fin_ss, fin_rs):
     rows2, head = qb.shape[1], qb.shape[2]
     tok = kb.shape[1]
     sub = tok // 4
@@ -102,7 +102,7 @@
         load.start()
 
     barrier = pltpu.get_barrier_semaphore()
-    peers = [partner] + [dev(y, wrap(x + d), c) for d in (1, 2, 3)] + [dev(wrap(y + d), x, c) for d in (1, 2, 3)]
+    peers = [partner] + [dev(y, wrap(x + d), c) for d in (1, 3)] + [dev(wrap(y + d), x, c) for d in (1, 3)]
     for peer in peers:
         pl.semaphore_signal(barrier, inc=1, device_id={'cp': peer}, device_id_type=MESH)
     pl.semaphore_wait(barrier, len(peers))
@@ -119,22 +119,46 @@
         for p in kv_pair(slot, kv_s3, partner):
             p.wait_recv()
 
-    def q_trio(row, dst_row):
+    def q_trio(row, dst_row, relayed=0):
         device = dev(dst_row, x, c)
-        return tuple(copy(b.at[row], b.at[row], q_ss.at[dst_row, i], q_rs.at[row, i], device)
+        return tuple(copy(b.at[row], b.at[row], q_ss.at[4 * relayed + dst_row, i], q_rs.at[row, i], device)
                      for i, b in enumerate((qb, dob, stb)))
+
+    def q_wait(row):
+        for p in q_trio(row, row):
+            p.wait_recv()
+
+    def kv_onward(slot, taken, toward):
+        buf = kb if toward == 0 else vb
+        return copy(buf.at[slot], buf.at[slot], kv_s5.at[2 * taken + toward], kv_rs.at[slot, toward],
+                    dev(y, wrap(x + (1 if toward == 0 else 3)), c))
 
     def par_copy(slot, idx):
         return copy(dkv.at[slot], par.at[idx], par_ss.at[idx], par_rs.at[idx], partner)
 
-    def ici_copy(slot, xs, cls):
-        return copy(dkv.at[slot], ici.at[4 * cls + x], ici_ss.at[4 * cls + xs], ici_rs.at[4 * cls + x], dev(y, xs, c))
-
-    def ici_wait(cls, xs):
-        copy(dkv.at[own], ici.at[4 * cls + xs], ici_ss.at[4 * cls + xs], ici_rs.at[4 * cls + xs], partner).wait_recv()
+    def ici_copy(slot, cls, side_in):
+        device = dev(y, jnp.where(side_in == 0, wrap(x + 1), wrap(x + 3)), c)
+        return copy(dkv.at[slot], ici.at[2 * cls + side_in], ici_ss.at[2 * cls + side_in],
+                    ici_rs.at[2 * cls + side_in], device)
+
+    def half_copy(slot, cls, h):
+        return copy(dkv.at[slot, h], half.at[2 * cls + h], half_ss.at[2 * cls + h], half_rs.at[2 * cls + h],
+                    dev(y, wrap(x + (1 if h == 0 else 3)), c))
 
     def dq_copy(row):
-        return copy(dqa.at[row], dqr.at[y], dq_ss.at[row], dq_rs.at[y], dev(row, x, c))
+        up = row == y + 1
+        dst = jnp.where(y == 3, jnp.where(row == 1, 0, 2), jnp.where(row == y + 3, 3, y + 1))
+        place = jnp.where(up, 1, jnp.where(jnp.logical_or(row == y + 3, row == y - 1), 2, 0))
+        return copy(dqa.at[row], dqr.at[place], dq_ss.at[row], dq_rs.at[place], dev(dst, x, c))
+
+    def dq_take(row, place):
+        copy(dqa.at[row], dqr.at[place], dq_ss.at[0], dq_rs.at[place], partner).wait_recv()
+
+        def body(i, carry):
+            part = pl.ds(pl.multiple_of(i * sub, sub), sub)
+            dqa[row, part, :] += dqr[place, part, :]
+            return carry
+        lax.fori_loop(0, rows2 // sub, body, 0)
 
     def fin_copy():
         return copy(dkv.at[8 + x], fin, fin_ss, fin_rs, mirror)
@@ -142,7 +166,7 @@
     for load in loads[:2]:
         load.wait()
     start(kv_pair(own, kv_s1.at[0], partner))
-    for d in (1, 3, 2):
+    for d in (1, 3):
         start(kv_pair(own, kv_s1.at[d], dev(y, wrap(x + d), c)))
 
     def give_copy():
@@ -156,7 +180,7 @@
 
     for load in loads[2:]:
         load.wait()
-    for d in (1, 3, 2):
+    for d in (1, 3):
         dst = wrap(y + d)
 
         @pl.when(feeds(dst, y))
@@ -186,7 +210,7 @@
         stats = stb[row, :, part].T
         power = logits * exp_scale - stats[:, 0:1]
         if masked:
-            r = lax.broadcasted_iota(jnp.int32, power.shape, 0) + u * sub
+            r = (lax.broadcasted_iota(jnp.int32, power.shape, 0) + u * sub) // 2
             power = jnp.where(lax.broadcasted_iota(jnp.int32, power.shape, 1) <= r, power, -1e30)
         prob = jnp.exp2(power)
         d_score = (prob * (d_prob - stats[:, 1:2])).astype(BF16)
@@ -196,34 +220,45 @@
         dqa[row, part, :] += jnp.dot(d_score, k_t, preferred_element_type=F32)
 
     def full_task(row, slot):
-        def head_loop(g, carry):
+        def half_loop(g, carry):
             for u in range(4):
-                piece(row, slot, pl.multiple_of(g * tok + u * sub, sub), tok, u, False)
+                piece(row, slot, pl.multiple_of((4 * g + u) * sub, sub), tok, 0, False)
             return carry
-        lax.fori_loop(0, 2, head_loop, 0)
+        lax.fori_loop(0, 2, half_loop, 0)
 
     def diag_task():
-        def head_loop(g, carry):
-            for u in range(4):
-                piece(y, own, pl.multiple_of(g * tok + u * sub, sub), (u + 1) * sub, u, True)
-            return carry
-        lax.fori_loop(0, 2, head_loop, 0)
-
-    def add_into(slot, other, oidx):
+        for u in range(8):
+            piece(y, own, u * sub, (u // 2 + 1) * sub, u, True)
+
+    def add_into(slot, h, other):
         def body(i, carry):
             part = pl.ds(pl.multiple_of(i * 32, 32), 32)
-            for h in range(2):
-                dkv[slot, h, part, :] += other[oidx, h, part, :]
+            dkv[slot, h, part, :] += other[part, :]
             return carry
         lax.fori_loop(0, head // 32, body, 0)
 
-    def reduce_chip(slot, xs, idx, cls):
+    def meets(xx, xs, cc):
+        return jnp.logical_or(jnp.logical_not(local_only(y, xs, cc)), xx >= xs)
+
+    def sum_chip(slot, xs, idx, cls):
         par_copy(slot, idx).wait_recv()
-        add_into(slot, par, idx)
-
-        @pl.when(xs != x)
-        def _():
-            ici_copy(slot, xs, cls).start()
+        for h in range(2):
+            add_into(slot, h, par.at[idx, h])
+
+        @pl.when(xs == wrap(x + 2))
+        def _():
+            for h in range(2):
+                half_copy(slot, cls, h).start()
+
+    def pass_on(slot, xs, cls, joined):
+        for h in range(2):
+            @pl.when(xs == wrap(x + (1 if h == 0 else 3)))
+            def _():
+                @pl.when(joined)
+                def _():
+                    half_copy(slot, cls, h).wait_recv()
+                    add_into(slot, h, half.at[2 * cls + h])
+                ici_copy(slot, cls, h).start()
 
     transpose_queries(y)
     diag_task()
@@ -232,19 +267,25 @@
     def _():
         kv_wait(8 + x)
         start(kv_pair(8 + x, kv_s4.at[0], partner))
-        for d in (1, 3, 2):
+        for d in (1, 3):
             start(kv_pair(8 + x, kv_s4.at[d], dev(y, wrap(x + d), c)))
 
-    def after_diag(mine):
+    def after_diag(stage):
         for xs in range(4):
-            cc = c if mine else 1 - c
-
-            @pl.when(jnp.logical_and(local_only(y, xs, cc), xs <= x))
-            def _():
-                if mine:
-                    reduce_chip(2 * xs + c, xs, xs, 0)
+            cc = 1 - c if stage == 0 else c
+            alone = local_only(y, xs, cc)
+
+            @pl.when(jnp.logical_and(alone, xs <= x if stage < 2 else jnp.logical_or(xs <= x, (xs + 2) % 4 >= xs)))
+            def _():
+                if stage == 0:
+                    par_copy(2 * xs + 1 - c, xs).start()
+                elif stage == 1:
+                    sum_chip(2 * xs + c, xs, xs, 0)
                 else:
-                    par_copy(2 * xs + 1 - c, xs).start()
+                    pass_on(2 * xs + c, xs, 0, (xs + 2) % 4 >= xs)
+
+    def taken_at(xs):
+        return jnp.logical_or(y == 3, jnp.logical_and(y == 2, xs < 2))
 
     def step(t, carry):
         half = t // 2
@@ -258,29 +299,66 @@
         slot = jnp.where(first, 2 * x_d + c_d, slot_u)
         row = jnp.where(first, y, field(T_Q, 2, u))
 
-        @pl.when(first)
+        later = jnp.logical_not(first)
+
+        @pl.when(jnp.logical_and(first, mate == 1))
         def _():
             kv_wait(slot)
 
-            @pl.when(mate == 0)
-            def _():
-                start(kv_pair(slot, kv_s2.at[x_d], partner))
-
-        later = jnp.logical_not(first)
+        @pl.when(t == 2)
+        def _():
+            for toward, dd in ((0, 3), (1, 1)):
+                near = 2 * wrap(x + dd) + c
+                kv_wait(near)
+                kv_onward(near, 0, toward).start()
+                start(kv_pair(near, kv_s2.at[wrap(x + dd)], partner))
+
+        @pl.when(t == 6)
+        def _():
+            kv_wait(slot)
+            start(kv_pair(slot, kv_s2.at[x_d], partner))
+
+        @pl.when(jnp.logical_and(t == 5, y == 0))
+        def _():
+            q_wait(3)
+            start(q_trio(3, 1, 1))
+            q_wait(1)
+            start(q_trio(1, 3, 1))
+
+        @pl.when(jnp.logical_and(t == 5, y == 1))
+        def _():
+            q_wait(2)
+            start(q_trio(2, 0, 1))
+
+        @pl.when(jnp.logical_and(t == 7, c == 0))
+        def _():
+            for toward, dd in ((0, 3), (1, 1)):
+                near = wrap(x + dd)
+
+                @pl.when(taken_at(near))
+                def _():
+                    kv_wait(8 + near)
+                    kv_onward(8 + near, 1, toward).start()
+                    start(kv_pair(8 + near, kv_s2.at[4 + near], partner))
 
         @pl.when(jnp.logical_and(later, field(T_QFIRST, 1, u) == 1))
         def _():
-            for p in q_trio(row, row):
-                p.wait_recv()
+            relayed = jnp.logical_or(jnp.logical_and(y == 0, row != 2), jnp.logical_and(y == 1, row == 2))
+
+            @pl.when(jnp.logical_not(relayed))
+            def _():
+                q_wait(row)
             transpose_queries(row)
 
         @pl.when(jnp.logical_and(later, field(T_TAKEN, 1, u) == 1))
         def _():
-            @pl.when(jnp.logical_or(c == 1, xs != x))
+            far = xs == wrap(x + 2)
+
+            @pl.when(jnp.logical_or(c == 1, far))
             def _():
                 kv_wait(slot)
 
-            @pl.when(jnp.logical_and(c == 0, xs != x))
+            @pl.when(jnp.logical_and(c == 0, far))
             def _():
                 start(kv_pair(slot, kv_s2.at[4 + xs], partner))
 
@@ -288,16 +366,16 @@
         def _():
             full_task(row, slot)
 
-        @pl.when(t == 7)
-        def _():
-            after_diag(False)
-
-        @pl.when(t == 9)
-        def _():
-            after_diag(True)
+        for stage, when in ((0, 7), (1, 9), (2, 13)):
+            @pl.when(t == when)
+            def _():
+                after_diag(stage)
 
         @pl.when(jnp.logical_and(later, field(T_QLAST, 1, u) == 1))
         def _():
+            @pl.when(row == y + 1)
+            def _():
+                dq_take(row, 0)
             dq_copy(row).start()
 
         done = field(T_KVLAST, 1, u) == 1
@@ -311,7 +389,8 @@
 
         @pl.when(jnp.logical_and(u > 0, jnp.logical_and(field(T_KVLAST, 1, before) == 1, c == resp_b)))
         def _():
-            reduce_chip(slot_b, xs_b, idx_b, idx_b // 4)
+            sum_chip(slot_b, xs_b, idx_b, idx_b // 4)
+            pass_on(slot_b, xs_b, idx_b // 4, True)
         return carry
 
     lax.fori_loop(1, 8 + N_TASK, step, 0)
@@ -320,46 +399,41 @@
 
     @pl.when(c == resp_b)
     def _():
-        reduce_chip(slot_b, xs_b, idx_b, idx_b // 4)
+        sum_chip(slot_b, xs_b, idx_b, idx_b // 4)
+        pass_on(slot_b, xs_b, idx_b // 4, True)
+
+    def from_side(slot, cls, side_in):
+        ici_copy(slot, cls, side_in).wait_recv()
+        for h in range(2):
+            add_into(slot, h, ici.at[2 * cls + side_in, h])
 
     @pl.when(takes)
     def _():
-        for d in (1, 3, 2):
-            ici_wait(1, wrap(x + d))
-            add_into(8 + x, ici, 4 + wrap(x + d))
+        for side_in in range(2):
+            from_side(8 + x, 1, side_in)
         fin_copy().start()
 
-    for d in (1, 3, 2):
-        xs = wrap(x + d)
-
-        @pl.when(jnp.logical_or(jnp.logical_not(local_only(y, x, c)), xs > x))
-        def _():
-            ici_wait(0, xs)
-            add_into(own, ici, xs)
-
-    for d in (1, 3, 2):
-        src = wrap(y + d)
-
-        @pl.when(feeds(src, y))
-        def _():
-            copy(dqa.at[y], dqr.at[src], dq_ss.at[src], dq_rs.at[src], partner).wait_recv()
-
-            def body(i, carry):
-                part = pl.ds(pl.multiple_of(i * sub, sub), sub)
-                dqa[y, part, :] += dqr[src, part, :]
-                return carry
-            lax.fori_loop(0, rows2 // sub, body, 0)
+    for side_in in range(2):
+        near = wrap(x + (3 if side_in == 0 else 1))
+
+        @pl.when(jnp.logical_or(meets(near, x, c), meets(wrap(x + 2), x, c)))
+        def _():
+            from_side(own, 0, side_in)
+
+    @pl.when(y >= 1)
+    def _():
+        dq_take(y, 1)
+
+    @pl.when(y >= 2)
+    def _():
+        dq_take(y, 2)
 
     @pl.when(gives)
     def _():
         fin_copy().wait_recv()
 
-        def body(i, carry):
-            part = pl.ds(pl.multiple_of(i * 32, 32), 32)
-            for h in range(2):
-                dkv[own, h, part, :] += fin[h, part, :]
-            return carry
-        lax.fori_loop(0, head // 32, body, 0)
+        for h in range(2):
+            add_into(own, h, fin.at[h])
 
     def out_q(i, carry):
         part = pl.ds(pl.multiple_of(i * sub, sub), sub)
@@ -376,19 +450,32 @@
         for p in pair:
             p.wait_send()
 
-    for d in range(4):
+    for d in (0, 1, 3):
         sent(kv_pair(own, kv_s1.at[d], partner))
+    for h in range(2):
+        kv_onward(own, 0, h).wait_send()
     for d in (1, 2, 3):
         sent(kv_pair(own, kv_s2.at[wrap(x + d)], partner))
+    for d in (1, 3):
         dst = wrap(y + d)
 
         @pl.when(feeds(dst, y))
         def _():
             sent(q_trio(y, dst))
 
-        @pl.when(feeds(y, dst))
-        def _():
-            dq_copy(dst).wait_send()
+    @pl.when(y == 0)
+    def _():
+        sent(q_trio(3, 1, 1))
+        sent(q_trio(1, 3, 1))
+
+    @pl.when(y == 1)
+    def _():
+        sent(q_trio(2, 0, 1))
+
+    for row in (1, 2, 3):
+        @pl.when(jnp.logical_and(row != y, feeds(y, row)))
+        def _():
+            dq_copy(row).wait_send()
 
     @pl.when(gives)
     def _():
@@ -396,29 +483,47 @@
 
     @pl.when(takes)
     def _():
-        for d in range(4):
+        for d in (0, 1, 3):
             sent(kv_pair(8 + x, kv_s4.at[d], partner))
         fin_copy().wait_send()
 
     for xs in range(4):
-        has_taken = jnp.logical_or(y == 3, y == 2) if xs < 2 else y == 3
-
-        @pl.when(jnp.logical_or(jnp.logical_not(local_only(y, xs, 1 - c)), xs <= x))
+        @pl.when(meets(x, xs, 1 - c))
         def _():
             par_copy(2 * xs + 1 - c, xs).wait_send()
 
-        @pl.when(jnp.logical_and(xs != x, jnp.logical_or(jnp.logical_not(local_only(y, xs, c)), xs < x)))
-        def _():
-            ici_copy(2 * xs + c, xs, 0).wait_send()
-
-        @pl.when(jnp.logical_and(c == 1, has_taken))
+        @pl.when(jnp.logical_and(c == 1, taken_at(xs)))
         def _():
             par_copy(8 + xs, 4 + xs).wait_send()
 
-        @pl.when(jnp.logical_and(jnp.logical_and(c == 0, xs != x), has_taken))
+        @pl.when(jnp.logical_and(jnp.logical_and(c == 0, xs != x), taken_at(xs)))
         def _():
             sent(kv_pair(8 + xs, kv_s2.at[4 + xs], partner))
-            ici_copy(8 + xs, xs, 1).wait_send()
+
+    far = wrap(x + 2)
+    for h in range(2):
+        behind = wrap(x + (3 if h == 0 else 1))
+        ahead = wrap(x + (1 if h == 0 else 3))
+
+        @pl.when(jnp.logical_and(c == 0, taken_at(behind)))
+        def _():
+            kv_onward(8 + x, 1, h).wait_send()
+
+        @pl.when(meets(x, far, c))
+        def _():
+            half_copy(own, 0, h).wait_send()
+
+        @pl.when(jnp.logical_or(meets(x, ahead, c), meets(behind, ahead, c)))
+        def _():
+            ici_copy(own, 0, h).wait_send()
+
+        @pl.when(jnp.logical_and(c == 0, taken_at(far)))
+        def _():
+            half_copy(own, 1, h).wait_send()
+
+        @pl.when(jnp.logical_and(c == 0, taken_at(ahead)))
+        def _():
+            ici_copy(own, 1, h).wait_send()
 
 
 def solution(mesh):
@@ -432,10 +537,10 @@
         scale = head ** -0.5
         rows2 = tok * heads
         delta = jnp.sum(d_out.astype(F32) * fwd_out.astype(F32), axis=-1)
-        stats = jnp.stack([lse_row * math.log2(math.e), delta]).transpose(0, 2, 1).reshape(2, rows2)
+        stats = jnp.stack([lse_row * math.log2(math.e), delta]).reshape(2, rows2)
         stats = jnp.pad(stats, ((0, 6), (0, 0)))
-        q_rows = q_tok.transpose(1, 0, 2).reshape(rows2, head)
-        do_rows = d_out.transpose(1, 0, 2).reshape(rows2, head)
+        q_rows = q_tok.reshape(rows2, head)
+        do_rows = d_out.reshape(rows2, head)
         hbm = pl.BlockSpec(memory_space=pl.ANY)
         vmem = pl.BlockSpec(memory_space=pltpu.VMEM)
         dma = pltpu.SemaphoreType.DMA
@@ -449,14 +554,15 @@
                 pltpu.VMEM((4, rows2, head), BF16), pltpu.VMEM((4, rows2, head), BF16), pltpu.VMEM((4, 8, rows2), F32),
                 pltpu.VMEM((4, head, rows2), BF16), pltpu.VMEM((4, head, rows2), BF16),
                 pltpu.VMEM((12, tok, head), BF16), pltpu.VMEM((12, tok, head), BF16),
-                pltpu.VMEM((4, rows2, head), F32), pltpu.VMEM((12, 2, head, tok), F32), pltpu.VMEM((4, rows2, head), F32),
-                pltpu.VMEM((8, 2, head, tok), F32), pltpu.VMEM((8, 2, head, tok), F32), pltpu.VMEM((2, head, tok), F32),
-                dma((5,)), dma((4, 3)), dma((4, 3)), dma((4, 2)), dma((8, 2)), dma((2,)), dma((4, 2)), dma((12, 2)),
-                dma((8,)), dma((8,)), dma((8,)), dma((8,)), dma((4,)), dma((4,)), dma, dma,
+                pltpu.VMEM((4, rows2, head), F32), pltpu.VMEM((12, 2, head, tok), F32), pltpu.VMEM((3, rows2, head), F32),
+                pltpu.VMEM((8, 2, head, tok), F32), pltpu.VMEM((4, 2, head, tok), F32), pltpu.VMEM((4, head, tok), F32),
+                pltpu.VMEM((2, head, tok), F32),
+                dma((5,)), dma((8, 3)), dma((4, 3)), dma((4, 2)), dma((8, 2)), dma((2,)), dma((4, 2)), dma((4,)), dma((12, 2)),
+                dma((8,)), dma((8,)), dma((4,)), dma((4,)), dma((4,)), dma((4,)), dma((4,)), dma((3,)), dma, dma,
             ],
             compiler_params=pltpu.CompilerParams(collective_id=0, has_side_effects=True, vmem_limit_bytes=66 * 10 ** 6),
             name='attn_grad',
         )(q_rows, do_rows, stats, k_tok, v_tok)
-        return gq.reshape(heads, tok, head).transpose(1, 0, 2), gk, gv
+        return gq.reshape(tok, heads, head), gk, gv
 
     return jax.shard_map(local_fn, mesh=mesh, in_specs=(row_spec,) * 6, out_specs=(row_spec,) * 3, check_vma=False)

time: 168 us -> 187 us (1.11)
  the two profiles are of different devices: /device:TPU:98 before, /device:TPU:122 now
where the time goes in v2:
time: 187 us
  Pallas kernels  178 us (95%)
  local copies, waits for them, and re-layouts  5.48 us (3%)
  other arithmetic  2.6 us (1%)
    pallas_call x1, Pallas kernels, local_fn(): pl.pallas_call(functools.partial(attn_grad_kernel, side, scale), out_shap...  178 us
    unnamed x11, local copies, waits for them, and re-layouts  4.63 us

profile of v2, /device:TPU:122, one launch (start us, length us, event | category | flops | bytes accessed | tf_op | source)
XLA Modules:
  0.0 187.1 jit_solution(16413018645677458866)
XLA Ops:
  0.6 0.7 broadcast_multiply_fusion
  1.3 0.0 copy-start
  1.3 0.0 copy-start.1
  1.3 0.2 copy.10
  1.6 0.3 stack.9
  1.9 0.5 copy-done
  2.4 0.2 copy-done.1
  2.5 1.2 multiply_reduce_fusion
  3.8 0.3 stack.10
  4.1 0.7 select_maximum_fusion.st_hbm
  4.7 178.3 %attn_grad.1 = (bf16[2048,128]{1,0:T(8,128)(2,1)}, bf16[1024,128]{1,0:T(8,128)(2,1)}, bf16[1024,128]{1,0:T(8,128)(2,1)}) custom-call(bf16[2048,128]{1,0:T(8,128)(2,1)} %bitcast.4, bf16[2048,128]{1,0:T(8,128)(2,1)} %bitcast.3, f32[8,2048]{1,0:T(8,128)} %select_maximum_fusion.st_hbm, bf16[1024,128]{1,0:T(8,128)(2,1)} %k_hbm.1, bf16[1024,128]{1,0:T(8,128)(2,1)} %v_hbm.1), custom_call_target="tpu_custom_call" | custom-call | tf_op jit(solution)/shard_map/attn_grad/pallas_call | solution.py:547
  183.1 0.0 copy-start.3
  183.1 2.2 %copy.14 = bf16[1024,2,128]{2,1,0:T(2,128)(2,1)} copy(bf16[1024,2,128]{2,1,0:T(2,128)(2,1)} %bitcast.5) | data formatting | bytes 1048576
  185.3 0.0 copy-done.3
  185.3 0.0 copy-start.2
  185.3 0.7 copy.15
  186.0 0.3 copy-done.2
  186.4 0.7 copy.16
Async XLA Ops:
  1.3 1.0 copy-start
  1.3 1.2 copy-start.1
  183.1 2.2 %copy-start.3 = (bf16[1024,128]{1,0:T(8,128)(2,1)S(1)}, bf16[1024,128]{1,0:T(8,128)(2,1)}, u32[]{:S(2)}) copy-start(bf16[1024,128]{1,0:T(8,128)(2,1)} %get-tuple-element.13) | copy-start | bytes 786436
  185.3 1.0 copy-start.2

commit v3 on v2

--- a/solution.py
+++ b/solution.py
@@ -22,6 +22,7 @@
     + [(q, dx, 0, 2) for q in (1, 2, 3) for dx in (3, 0)],
 )
 N_TASK = 12
+DELAY = 2
 
 
 def pack(rows, bits):
@@ -119,13 +120,13 @@
         for p in kv_pair(slot, kv_s3, partner):
             p.wait_recv()
 
-    def q_trio(row, dst_row, relayed=0):
+    def q_trio(row, dst_row, relayed=0, parts=(0, 1, 2)):
         device = dev(dst_row, x, c)
         return tuple(copy(b.at[row], b.at[row], q_ss.at[4 * relayed + dst_row, i], q_rs.at[row, i], device)
-                     for i, b in enumerate((qb, dob, stb)))
-
-    def q_wait(row):
-        for p in q_trio(row, row):
+                     for i, b in enumerate((qb, dob, stb)) if i in parts)
+
+    def q_wait(row, parts=(0, 1, 2)):
+        for p in q_trio(row, row, 0, parts):
             p.wait_recv()
 
     def kv_onward(slot, taken, toward):
@@ -136,32 +137,34 @@
     def par_copy(slot, idx):
         return copy(dkv.at[slot], par.at[idx], par_ss.at[idx], par_rs.at[idx], partner)
 
-    def ici_copy(slot, cls, side_in):
+    def ici_copy(slot, cls, side_in, h):
         device = dev(y, jnp.where(side_in == 0, wrap(x + 1), wrap(x + 3)), c)
-        return copy(dkv.at[slot], ici.at[2 * cls + side_in], ici_ss.at[2 * cls + side_in],
-                    ici_rs.at[2 * cls + side_in], device)
+        return copy(dkv.at[slot, h], ici.at[2 * cls + side_in, h], ici_ss.at[2 * cls + side_in, h],
+                    ici_rs.at[2 * cls + side_in, h], device)
 
     def half_copy(slot, cls, h):
         return copy(dkv.at[slot, h], half.at[2 * cls + h], half_ss.at[2 * cls + h], half_rs.at[2 * cls + h],
                     dev(y, wrap(x + (1 if h == 0 else 3)), c))
 
-    def dq_copy(row):
+    def dq_copy(row, h):
         up = row == y + 1
         dst = jnp.where(y == 3, jnp.where(row == 1, 0, 2), jnp.where(row == y + 3, 3, y + 1))
         place = jnp.where(up, 1, jnp.where(jnp.logical_or(row == y + 3, row == y - 1), 2, 0))
-        return copy(dqa.at[row], dqr.at[place], dq_ss.at[row], dq_rs.at[place], dev(dst, x, c))
-
-    def dq_take(row, place):
-        copy(dqa.at[row], dqr.at[place], dq_ss.at[0], dq_rs.at[place], partner).wait_recv()
+        part = pl.ds(h * tok, tok)
+        return copy(dqa.at[row, part], dqr.at[place, part], dq_ss.at[row, h], dq_rs.at[place, h], dev(dst, x, c))
+
+    def dq_take(row, place, h):
+        half_rows = pl.ds(h * tok, tok)
+        copy(dqa.at[row, half_rows], dqr.at[place, half_rows], dq_ss.at[0, h], dq_rs.at[place, h], partner).wait_recv()
 
         def body(i, carry):
-            part = pl.ds(pl.multiple_of(i * sub, sub), sub)
+            part = pl.ds(pl.multiple_of(h * tok + i * sub, sub), sub)
             dqa[row, part, :] += dqr[place, part, :]
             return carry
-        lax.fori_loop(0, rows2 // sub, body, 0)
-
-    def fin_copy():
-        return copy(dkv.at[8 + x], fin, fin_ss, fin_rs, mirror)
+        lax.fori_loop(0, tok // sub, body, 0)
+
+    def fin_copy(h):
+        return copy(dkv.at[8 + x, h], fin.at[h], fin_ss.at[h], fin_rs.at[h], mirror)
 
     for load in loads[:2]:
         load.wait()
@@ -258,7 +261,8 @@
                 def _():
                     half_copy(slot, cls, h).wait_recv()
                     add_into(slot, h, half.at[2 * cls + h])
-                ici_copy(slot, cls, h).start()
+                for part in range(2):
+                    ici_copy(slot, cls, h, part).start()
 
     transpose_queries(y)
     diag_task()
@@ -318,17 +322,18 @@
             kv_wait(slot)
             start(kv_pair(slot, kv_s2.at[x_d], partner))
 
-        @pl.when(jnp.logical_and(t == 5, y == 0))
-        def _():
-            q_wait(3)
-            start(q_trio(3, 1, 1))
-            q_wait(1)
-            start(q_trio(1, 3, 1))
-
-        @pl.when(jnp.logical_and(t == 5, y == 1))
-        def _():
-            q_wait(2)
-            start(q_trio(2, 0, 1))
+        for when, parts in ((3, (0,)), (5, (1, 2))):
+            @pl.when(jnp.logical_and(t == when, y == 0))
+            def _():
+                q_wait(3, parts)
+                start(q_trio(3, 1, 1, parts))
+                q_wait(1, parts)
+                start(q_trio(1, 3, 1, parts))
+
+            @pl.when(jnp.logical_and(t == when, y == 1))
+            def _():
+                q_wait(2, parts)
+                start(q_trio(2, 0, 1, parts))
 
         @pl.when(jnp.logical_and(t == 7, c == 0))
         def _():
@@ -366,17 +371,18 @@
         def _():
             full_task(row, slot)
 
-        for stage, when in ((0, 7), (1, 9), (2, 13)):
+        for stage, when in ((0, 12), (1, 14), (2, 16)):
             @pl.when(t == when)
             def _():
                 after_diag(stage)
 
         @pl.when(jnp.logical_and(later, field(T_QLAST, 1, u) == 1))
         def _():
-            @pl.when(row == y + 1)
-            def _():
-                dq_take(row, 0)
-            dq_copy(row).start()
+            for h in range(2):
+                @pl.when(row == y + 1)
+                def _():
+                    dq_take(row, 0, h)
+                dq_copy(row, h).start()
 
         done = field(T_KVLAST, 1, u) == 1
 
@@ -384,55 +390,61 @@
         def _():
             par_copy(slot, idx).start()
 
-        before = jnp.maximum(u - 1, 0)
-        slot_b, xs_b, idx_b, resp_b = decode(before)
-
-        @pl.when(jnp.logical_and(u > 0, jnp.logical_and(field(T_KVLAST, 1, before) == 1, c == resp_b)))
-        def _():
-            sum_chip(slot_b, xs_b, idx_b, idx_b // 4)
+        def finished(back, action):
+            before = jnp.maximum(u - back, 0)
+            slot_b, xs_b, idx_b, resp_b = decode(before)
+
+            @pl.when(jnp.logical_and(u >= back, jnp.logical_and(field(T_KVLAST, 1, before) == 1, c == resp_b)))
+            def _():
+                action(slot_b, xs_b, idx_b)
+
+        finished(1, lambda slot_b, xs_b, idx_b: sum_chip(slot_b, xs_b, idx_b, idx_b // 4))
+        finished(1 + DELAY, lambda slot_b, xs_b, idx_b: pass_on(slot_b, xs_b, idx_b // 4, True))
+        return carry
+
+    lax.fori_loop(1, 8 + N_TASK, step, 0)
+
+    for u_b in range(N_TASK - 1 - DELAY, N_TASK):
+        slot_b, xs_b, idx_b, resp_b = decode(jnp.int32(u_b))
+
+        @pl.when(jnp.logical_and(field(T_KVLAST, 1, u_b) == 1, c == resp_b))
+        def _():
+            if u_b == N_TASK - 1:
+                sum_chip(slot_b, xs_b, idx_b, idx_b // 4)
             pass_on(slot_b, xs_b, idx_b // 4, True)
-        return carry
-
-    lax.fori_loop(1, 8 + N_TASK, step, 0)
-
-    slot_b, xs_b, idx_b, resp_b = decode(jnp.int32(N_TASK - 1))
-
-    @pl.when(c == resp_b)
-    def _():
-        sum_chip(slot_b, xs_b, idx_b, idx_b // 4)
-        pass_on(slot_b, xs_b, idx_b // 4, True)
-
-    def from_side(slot, cls, side_in):
-        ici_copy(slot, cls, side_in).wait_recv()
+
+    def from_side(slot, cls, side_in, h):
+        ici_copy(slot, cls, side_in, h).wait_recv()
+        add_into(slot, h, ici.at[2 * cls + side_in, h])
+
+    @pl.when(takes)
+    def _():
         for h in range(2):
-            add_into(slot, h, ici.at[2 * cls + side_in, h])
-
-    @pl.when(takes)
-    def _():
-        for side_in in range(2):
-            from_side(8 + x, 1, side_in)
-        fin_copy().start()
+            for side_in in range(2):
+                from_side(8 + x, 1, side_in, h)
+            fin_copy(h).start()
 
     for side_in in range(2):
         near = wrap(x + (3 if side_in == 0 else 1))
 
         @pl.when(jnp.logical_or(meets(near, x, c), meets(wrap(x + 2), x, c)))
         def _():
-            from_side(own, 0, side_in)
-
-    @pl.when(y >= 1)
-    def _():
-        dq_take(y, 1)
-
-    @pl.when(y >= 2)
-    def _():
-        dq_take(y, 2)
+            for h in range(2):
+                from_side(own, 0, side_in, h)
+
+    for h in range(2):
+        @pl.when(y >= 1)
+        def _():
+            dq_take(y, 1, h)
+
+        @pl.when(y >= 2)
+        def _():
+            dq_take(y, 2, h)
 
     @pl.when(gives)
     def _():
-        fin_copy().wait_recv()
-
         for h in range(2):
+            fin_copy(h).wait_recv()
             add_into(own, h, fin.at[h])
 
     def out_q(i, carry):
@@ -475,7 +487,8 @@
     for row in (1, 2, 3):
         @pl.when(jnp.logical_and(row != y, feeds(y, row)))
         def _():
-            dq_copy(row).wait_send()
+            for h in range(2):
+                dq_copy(row, h).wait_send()
 
     @pl.when(gives)
     def _():
@@ -485,7 +498,8 @@
     def _():
         for d in (0, 1, 3):
             sent(kv_pair(8 + x, kv_s4.at[d], partner))
-        fin_copy().wait_send()
+        for h in range(2):
+            fin_copy(h).wait_send()
 
     for xs in range(4):
         @pl.when(meets(x, xs, 1 - c))
@@ -515,7 +529,8 @@
 
         @pl.when(jnp.logical_or(meets(x, ahead, c), meets(behind, ahead, c)))
         def _():
-            ici_copy(own, 0, h).wait_send()
+            for part in range(2):
+                ici_copy(own, 0, h, part).wait_send()
 
         @pl.when(jnp.logical_and(c == 0, taken_at(far)))
         def _():
@@ -523,7 +538,8 @@
 
         @pl.when(jnp.logical_and(c == 0, taken_at(ahead)))
         def _():
-            ici_copy(own, 1, h).wait_send()
+            for part in range(2):
+                ici_copy(own, 1, h, part).wait_send()
 
 
 def solution(mesh):
@@ -558,7 +574,7 @@
                 pltpu.VMEM((8, 2, head, tok), F32), pltpu.VMEM((4, 2, head, tok), F32), pltpu.VMEM((4, head, tok), F32),
                 pltpu.VMEM((2, head, tok), F32),
                 dma((5,)), dma((8, 3)), dma((4, 3)), dma((4, 2)), dma((8, 2)), dma((2,)), dma((4, 2)), dma((4,)), dma((12, 2)),
-                dma((8,)), dma((8,)), dma((4,)), dma((4,)), dma((4,)), dma((4,)), dma((4,)), dma((3,)), dma, dma,
+                dma((8,)), dma((8,)), dma((4, 2)), dma((4, 2)), dma((4,)), dma((4,)), dma((4, 2)), dma((3, 2)), dma((2,)), dma((2,)),
             ],
             compiler_params=pltpu.CompilerParams(collective_id=0, has_side_effects=True, vmem_limit_bytes=66 * 10 ** 6),
             name='attn_grad',

time: 187 us -> 164 us (0.88)
  the two profiles are of different devices: /device:TPU:122 before, /device:TPU:98 now
where the time goes in v3:
time: 164 us
  Pallas kernels  155 us (95%)
  local copies, waits for them, and re-layouts  5.48 us (3%)
  other arithmetic  2.6 us (2%)
    pallas_call x1, Pallas kernels, local_fn(): pl.pallas_call(functools.partial(attn_grad_kernel, side, scale), out_shap...  155 us
    unnamed x11, local copies, waits for them, and re-layouts  4.63 us

profile of v3, /device:TPU:98, one launch (start us, length us, event | category | flops | bytes accessed | tf_op | source)
XLA Modules:
  0.0 163.7 jit_solution(7736332063627523794)
XLA Ops:
  0.6 0.7 broadcast_multiply_fusion
  1.3 0.0 copy-start
  1.3 0.0 copy-start.1
  1.3 0.2 copy.10
  1.6 0.3 stack.9
  1.9 0.5 copy-done
  2.4 0.2 copy-done.1
  2.5 1.2 multiply_reduce_fusion
  3.8 0.3 stack.10
  4.1 0.7 select_maximum_fusion.st_hbm
  4.7 154.9 %attn_grad.1 = (bf16[2048,128]{1,0:T(8,128)(2,1)}, bf16[1024,128]{1,0:T(8,128)(2,1)}, bf16[1024,128]{1,0:T(8,128)(2,1)}) custom-call(bf16[2048,128]{1,0:T(8,128)(2,1)} %bitcast.4, bf16[2048,128]{1,0:T(8,128)(2,1)} %bitcast.3, f32[8,2048]{1,0:T(8,128)} %select_maximum_fusion.st_hbm, bf16[1024,128]{1,0:T(8,128)(2,1)} %k_hbm.1, bf16[1024,128]{1,0:T(8,128)(2,1)} %v_hbm.1), custom_call_target="tpu_custom_call" | custom-call | tf_op jit(solution)/shard_map/attn_grad/pallas_call | solution.py:563
  159.7 0.0 copy-start.3
  159.7 2.2 %copy.14 = bf16[1024,2,128]{2,1,0:T(2,128)(2,1)} copy(bf16[1024,2,128]{2,1,0:T(2,128)(2,1)} %bitcast.5) | data formatting | bytes 1048576
  161.9 0.0 copy-done.3
  161.9 0.0 copy-start.2
  161.9 0.7 copy.15
  162.6 0.3 copy-done.2
  163.0 0.7 copy.16
Async XLA Ops:
  1.3 1.0 copy-start
  1.3 1.2 copy-start.1
  159.7 2.2 %copy-start.3 = (bf16[1024,128]{1,0:T(8,128)(2,1)S(1)}, bf16[1024,128]{1,0:T(8,128)(2,1)}, u32[]{:S(2)}) copy-start(bf16[1024,128]{1,0:T(8,128)(2,1)} %get-tuple-element.13) | copy-start | bytes 786436
  161.9 1.0 copy-start.2

commit v4 on v3

--- a/solution.py
+++ b/solution.py
@@ -47,8 +47,8 @@
 T_TAKEN = pack([[f * int(e[3] == 2) for f, e in zip(first_use(r, lambda e: e[1:]), r)] for r in ROWS], 1)
 
 
-def attn_grad_kernel(side, scale, q_hbm, do_hbm, st_hbm, k_hbm, v_hbm, gq_ref, gk_ref, gv_ref,
-                     qb, dob, stb, qtb, dotb, kb, vb, dqa, dkv, dqr, par, ici, half, fin,
+def attn_grad_kernel(side, scale, q_hbm, do_hbm, o_hbm, lse_hbm, k_hbm, v_hbm, gq_ref, gk_ref, gv_ref,
+                     qb, dob, stb, ob, lseb, qtb, dotb, kb, vb, dqa, dkv, dqr, par, ici, half, fin,
                      ld_sem, q_ss, q_rs, kv_s1, kv_s2, kv_s3, kv_s4, kv_s5, kv_rs,
                      par_ss, par_rs, ici_ss, ici_rs, half_ss, half_rs, dq_ss, dq_rs, fin_ss, fin_rs):
     rows2, head = qb.shape[1], qb.shape[2]
@@ -98,7 +98,7 @@
     mirror = dev(3 - y, x, c)
 
     loads = [pltpu.make_async_copy(src, dst, ld_sem.at[i]) for i, (src, dst) in enumerate((
-        (k_hbm, kb.at[own]), (v_hbm, vb.at[own]), (q_hbm, qb.at[y]), (do_hbm, dob.at[y]), (st_hbm, stb.at[y])))]
+        (k_hbm, kb.at[own]), (v_hbm, vb.at[own]), (q_hbm, qb.at[y]), (do_hbm, dob.at[y]), (o_hbm, ob), (lse_hbm, lseb)))]
     for load in loads:
         load.start()
 
@@ -183,12 +183,16 @@
 
     for load in loads[2:]:
         load.wait()
-    for d in (1, 3):
-        dst = wrap(y + d)
-
-        @pl.when(feeds(dst, y))
-        def _():
-            start(q_trio(y, dst))
+
+    def feed(parts):
+        for d in (1, 3):
+            dst = wrap(y + d)
+
+            @pl.when(feeds(dst, y))
+            def _():
+                start(q_trio(y, dst, 0, parts))
+
+    feed((0, 1))
 
     def clear(ref, slots):
         def body(i, carry):
@@ -196,7 +200,22 @@
             return carry
         lax.fori_loop(0, slots, body, 0)
 
+    def row_stats():
+        stb[y] = jnp.zeros(stb.shape[1:], F32)
+        pair = (sub // 2, sub)
+        spread = (lax.broadcasted_iota(jnp.int32, pair, 1) // 2 == lax.broadcasted_iota(jnp.int32, pair, 0)).astype(F32)
+        even = lax.broadcasted_iota(jnp.int32, (1, sub), 1) % 2 == 0
+        for p in range(rows2 // sub):
+            part = pl.ds(p * sub, sub)
+            lse = lseb[:, pl.ds(p * sub // 2, sub // 2)] * math.log2(math.e)
+            lse = jnp.dot(lse, spread, precision=lax.Precision.HIGHEST, preferred_element_type=F32)
+            stb[y, 0:1, part] = jnp.where(even, lse[0:1], lse[1:2])
+            prod = dob[y, part, :].astype(F32) * ob[part, :].astype(F32)
+            stb[y, 1:2, part] = jnp.sum(prod.T, axis=0, keepdims=True)
+
+    row_stats()
     clear(dkv, dkv.shape[0])
+    feed((2,))
     clear(dqa, dqa.shape[0])
 
     def transpose_queries(row):
@@ -223,11 +242,8 @@
         dqa[row, part, :] += jnp.dot(d_score, k_t, preferred_element_type=F32)
 
     def full_task(row, slot):
-        def half_loop(g, carry):
-            for u in range(4):
-                piece(row, slot, pl.multiple_of((4 * g + u) * sub, sub), tok, 0, False)
-            return carry
-        lax.fori_loop(0, 2, half_loop, 0)
+        for u in range(rows2 // sub):
+            piece(row, slot, u * sub, tok, 0, False)
 
     def diag_task():
         for u in range(8):
@@ -552,33 +568,36 @@
         tok, heads, head = q_tok.shape
         scale = head ** -0.5
         rows2 = tok * heads
-        delta = jnp.sum(d_out.astype(F32) * fwd_out.astype(F32), axis=-1)
-        stats = jnp.stack([lse_row * math.log2(math.e), delta]).reshape(2, rows2)
-        stats = jnp.pad(stats, ((0, 6), (0, 0)))
         q_rows = q_tok.reshape(rows2, head)
         do_rows = d_out.reshape(rows2, head)
+        o_rows = fwd_out.reshape(rows2, head)
         hbm = pl.BlockSpec(memory_space=pl.ANY)
         vmem = pl.BlockSpec(memory_space=pltpu.VMEM)
-        dma = pltpu.SemaphoreType.DMA
+        slots = 3 * side
+        line, grid = pltpu.SemaphoreType.DMA((8,)), pltpu.SemaphoreType.DMA((slots, 3))
+        rows_low = pltpu.VMEM((side, rows2, head), BF16)
+        cols_low = pltpu.VMEM((side, head, rows2), BF16)
+        keys = pltpu.VMEM((slots, tok, head), BF16)
+
+        def sums(n):
+            return pltpu.VMEM((n, 2, head, tok), F32)
+
         gq, gk, gv = pl.pallas_call(
             functools.partial(attn_grad_kernel, side, scale),
             out_shape=[jax.ShapeDtypeStruct((rows2, head), BF16), jax.ShapeDtypeStruct((tok, head), BF16),
                        jax.ShapeDtypeStruct((tok, head), BF16)],
-            in_specs=[hbm] * 5,
+            in_specs=[hbm] * 6,
             out_specs=[vmem] * 3,
             scratch_shapes=[
-                pltpu.VMEM((4, rows2, head), BF16), pltpu.VMEM((4, rows2, head), BF16), pltpu.VMEM((4, 8, rows2), F32),
-                pltpu.VMEM((4, head, rows2), BF16), pltpu.VMEM((4, head, rows2), BF16),
-                pltpu.VMEM((12, tok, head), BF16), pltpu.VMEM((12, tok, head), BF16),
-                pltpu.VMEM((4, rows2, head), F32), pltpu.VMEM((12, 2, head, tok), F32), pltpu.VMEM((3, rows2, head), F32),
-                pltpu.VMEM((8, 2, head, tok), F32), pltpu.VMEM((4, 2, head, tok), F32), pltpu.VMEM((4, head, tok), F32),
-                pltpu.VMEM((2, head, tok), F32),
-                dma((5,)), dma((8, 3)), dma((4, 3)), dma((4, 2)), dma((8, 2)), dma((2,)), dma((4, 2)), dma((4,)), dma((12, 2)),
-                dma((8,)), dma((8,)), dma((4, 2)), dma((4, 2)), dma((4,)), dma((4,)), dma((4, 2)), dma((3, 2)), dma((2,)), dma((2,)),
+                rows_low, rows_low, pltpu.VMEM((side, 8, rows2), F32), pltpu.VMEM((rows2, head), BF16),
+                pltpu.VMEM((heads, tok), F32), cols_low, cols_low, keys, keys, pltpu.VMEM((side, rows2, head), F32),
+                sums(slots), pltpu.VMEM((3, rows2, head), F32), sums(8), sums(side), pltpu.VMEM((side, head, tok), F32),
+                pltpu.VMEM((2, head, tok), F32), line, grid, grid, grid, grid, line, grid, line, grid,
+                line, line, grid, grid, line, line, grid, grid, line, line,
             ],
             compiler_params=pltpu.CompilerParams(collective_id=0, has_side_effects=True, vmem_limit_bytes=66 * 10 ** 6),
             name='attn_grad',
-        )(q_rows, do_rows, stats, k_tok, v_tok)
+        )(q_rows, do_rows, o_rows, lse_row.T, k_tok, v_tok)
         return gq.reshape(tok, heads, head), gk, gv
 
     return jax.shard_map(local_fn, mesh=mesh, in_specs=(row_spec,) * 6, out_specs=(row_spec,) * 3, check_vma=False)

time: 164 us -> 165 us (level)
  Pallas kernels: 155 us -> 160 us
  other arithmetic: 2.6 us -> 0 us
    pallas_call x1, Pallas kernels: 155 us -> 160 us  [local_fn(): pl.pallas_call(functools.partial(attn_grad_kernel, side, scale), out_shap...]
    unnamed x11 -> x7, local copies, waits for them, and re-layouts: 4.63 us -> 3.99 us
where the time goes in v4:
time: 165 us
  Pallas kernels  160 us (97%)
  local copies, waits for them, and re-layouts  3.99 us (2%)
    pallas_call x1, Pallas kernels, local_fn(): pl.pallas_call(functools.partial(attn_grad_kernel, side, scale), out_shap...  160 us
    unnamed x7, local copies, waits for them, and re-layouts  3.99 us

profile of v4, /device:TPU:98, one launch (start us, length us, event | category | flops | bytes accessed | tf_op | source)
XLA Modules:
  0.0 164.7 jit_solution(8090456754107984933)
XLA Ops:
  0.6 160.1 %attn_grad.1 = (bf16[2048,128]{1,0:T(8,128)(2,1)}, bf16[1024,128]{1,0:T(8,128)(2,1)}, bf16[1024,128]{1,0:T(8,128)(2,1)}) custom-call(bf16[2048,128]{1,0:T(8,128)(2,1)} %bitcast.6, bf16[2048,128]{1,0:T(8,128)(2,1)} %bitcast.7, bf16[2048,128]{1,0:T(8,128)(2,1)} %bitcast.8, f32[2,1024]{1,0:T(2,128)} %bitcast.9, bf16[1024,128]{1,0:T(8,128)(2,1)} %k_hbm.1, ...), custom_call_target="tpu_custom_call" | custom-call | tf_op jit(solution)/shard_map/attn_grad/pallas_call | solution.py:585
  160.7 0.0 copy-start.1
  160.7 2.2 %copy.12 = bf16[1024,2,128]{2,1,0:T(2,128)(2,1)} copy(bf16[1024,2,128]{2,1,0:T(2,128)(2,1)} %bitcast.5) | data formatting | bytes 1048576
  163.0 0.0 copy-done.1
  163.0 0.0 copy-start
  163.0 0.7 copy.13
  163.7 0.3 copy-done
  164.0 0.7 copy.14
Async XLA Ops:
  160.7 2.2 %copy-start.1 = (bf16[1024,128]{1,0:T(8,128)(2,1)S(1)}, bf16[1024,128]{1,0:T(8,128)(2,1)}, u32[]{:S(2)}) copy-start(bf16[1024,128]{1,0:T(8,128)(2,1)} %get-tuple-element.13) | copy-start | bytes 786436
  163.0 1.0 copy-start

commit v5 on v4

--- a/solution.py
+++ b/solution.py
@@ -22,6 +22,9 @@
     + [(q, dx, 0, 2) for q in (1, 2, 3) for dx in (3, 0)],
 )
 N_TASK = 12
+SPLIT = 2
+WHOLE = N_TASK - SPLIT
+N_STEP = WHOLE + 2 * SPLIT
 DELAY = 2
 
 
@@ -85,6 +88,13 @@
         idx = jnp.where(taken, 4 + xs, xs)
         resp = jnp.where(taken, 0, kind)
         return slot, xs, idx, resp
+
+    def unit(v):
+        w = v - WHOLE
+        by_half = y < 3
+        which = jnp.where(by_half, lax.rem(w, 2), w // 2)
+        part = jnp.where(by_half, w // 2, lax.rem(w, 2))
+        return jnp.where(w < 0, v, WHOLE + which), jnp.maximum(part, 0), jnp.logical_or(w < 0, part == 1)
 
     def feeds(src, dst):
         return jnp.logical_or(src < dst, jnp.logical_and(src == 3, jnp.logical_and(dst > 0, dst < 3)))
@@ -241,9 +251,12 @@
         dkv[slot, 0, :, :width] += jnp.dot(qtb[row, :, part], d_score, preferred_element_type=F32)
         dqa[row, part, :] += jnp.dot(d_score, k_t, preferred_element_type=F32)
 
-    def full_task(row, slot):
-        for u in range(rows2 // sub):
-            piece(row, slot, u * sub, tok, 0, False)
+    def full_task(row, slot, first_half, end_half):
+        def half_loop(g, carry):
+            for u in range(tok // sub):
+                piece(row, slot, pl.multiple_of(g * tok + u * sub, sub), tok, 0, False)
+            return carry
+        lax.fori_loop(first_half, end_half, half_loop, 0)
 
     def diag_task():
         for u in range(8):
@@ -313,13 +326,16 @@
         x_d = wrap(x + d)
         mate = lax.rem(t, 2)
         c_d = jnp.where(mate == 0, c, 1 - c)
-        u = jnp.maximum(t - 8, 0)
+        v = jnp.maximum(t - 8, 0)
+        u, part, ends = unit(v)
+        whole = v < WHOLE
         first = t < 8
         slot_u, xs, idx, resp = decode(u)
         slot = jnp.where(first, 2 * x_d + c_d, slot_u)
         row = jnp.where(first, y, field(T_Q, 2, u))
 
         later = jnp.logical_not(first)
+        fresh = jnp.logical_and(later, whole)
 
         @pl.when(jnp.logical_and(first, mate == 1))
         def _():
@@ -362,7 +378,7 @@
                     kv_onward(8 + near, 1, toward).start()
                     start(kv_pair(8 + near, kv_s2.at[4 + near], partner))
 
-        @pl.when(jnp.logical_and(later, field(T_QFIRST, 1, u) == 1))
+        @pl.when(jnp.logical_and(fresh, field(T_QFIRST, 1, u) == 1))
         def _():
             relayed = jnp.logical_or(jnp.logical_and(y == 0, row != 2), jnp.logical_and(y == 1, row == 2))
 
@@ -371,7 +387,7 @@
                 q_wait(row)
             transpose_queries(row)
 
-        @pl.when(jnp.logical_and(later, field(T_TAKEN, 1, u) == 1))
+        @pl.when(jnp.logical_and(fresh, field(T_TAKEN, 1, u) == 1))
         def _():
             far = xs == wrap(x + 2)
 
@@ -385,32 +401,33 @@
 
         @pl.when(jnp.logical_or(later, 2 * x_d + c_d < own))
         def _():
-            full_task(row, slot)
+            full_task(row, slot, jnp.where(whole, 0, part), jnp.where(whole, 2, part + 1))
 
         for stage, when in ((0, 12), (1, 14), (2, 16)):
             @pl.when(t == when)
             def _():
                 after_diag(stage)
 
-        @pl.when(jnp.logical_and(later, field(T_QLAST, 1, u) == 1))
-        def _():
-            for h in range(2):
+        for h in range(2):
+            @pl.when(jnp.logical_and(jnp.logical_and(later, field(T_QLAST, 1, u) == 1), jnp.logical_or(whole, part == h)))
+            def _():
                 @pl.when(row == y + 1)
                 def _():
                     dq_take(row, 0, h)
                 dq_copy(row, h).start()
 
-        done = field(T_KVLAST, 1, u) == 1
+        done = jnp.logical_and(ends, field(T_KVLAST, 1, u) == 1)
 
         @pl.when(jnp.logical_and(later, jnp.logical_and(done, c != resp)))
         def _():
             par_copy(slot, idx).start()
 
         def finished(back, action):
-            before = jnp.maximum(u - back, 0)
+            before, _, ends_b = unit(jnp.maximum(v - back, 0))
             slot_b, xs_b, idx_b, resp_b = decode(before)
-
-            @pl.when(jnp.logical_and(u >= back, jnp.logical_and(field(T_KVLAST, 1, before) == 1, c == resp_b)))
+            ready = jnp.logical_and(ends_b, field(T_KVLAST, 1, before) == 1)
+
+            @pl.when(jnp.logical_and(v >= back, jnp.logical_and(ready, c == resp_b)))
             def _():
                 action(slot_b, xs_b, idx_b)
 
@@ -418,14 +435,15 @@
         finished(1 + DELAY, lambda slot_b, xs_b, idx_b: pass_on(slot_b, xs_b, idx_b // 4, True))
         return carry
 
-    lax.fori_loop(1, 8 + N_TASK, step, 0)
-
-    for u_b in range(N_TASK - 1 - DELAY, N_TASK):
-        slot_b, xs_b, idx_b, resp_b = decode(jnp.int32(u_b))
-
-        @pl.when(jnp.logical_and(field(T_KVLAST, 1, u_b) == 1, c == resp_b))
-        def _():
-            if u_b == N_TASK - 1:
+    lax.fori_loop(1, 8 + N_STEP, step, 0)
+
+    for v_b in range(N_STEP - 1 - DELAY, N_STEP):
+        u_b, _, ends_b = unit(jnp.int32(v_b))
+        slot_b, xs_b, idx_b, resp_b = decode(u_b)
+
+        @pl.when(jnp.logical_and(jnp.logical_and(ends_b, field(T_KVLAST, 1, u_b) == 1), c == resp_b))
+        def _():
+            if v_b == N_STEP - 1:
                 sum_chip(slot_b, xs_b, idx_b, idx_b // 4)
             pass_on(slot_b, xs_b, idx_b // 4, True)
 

time: 165 us -> 164 us (level)
  no operation moved by 1% of the time
where the time goes in v5:
time: 164 us; the launch traced here: 163 us
  Pallas kernels  159 us (97%)
  local copies, waits for them, and re-layouts  3.99 us (2%)
    pallas_call x1, Pallas kernels, local_fn(): pl.pallas_call(functools.partial(attn_grad_kernel, side, scale), out_shap...  159 us
    unnamed x7, local copies, waits for them, and re-layouts  3.99 us

profile of v5, /device:TPU:98, one launch (start us, length us, event | category | flops | bytes accessed | tf_op | source)
XLA Modules:
  0.0 163.4 jit_solution(1768879812205335725)
XLA Ops:
  0.6 158.8 %attn_grad.1 = (bf16[2048,128]{1,0:T(8,128)(2,1)}, bf16[1024,128]{1,0:T(8,128)(2,1)}, bf16[1024,128]{1,0:T(8,128)(2,1)}) custom-call(bf16[2048,128]{1,0:T(8,128)(2,1)} %bitcast.6, bf16[2048,128]{1,0:T(8,128)(2,1)} %bitcast.7, bf16[2048,128]{1,0:T(8,128)(2,1)} %bitcast.8, f32[2,1024]{1,0:T(2,128)} %bitcast.9, bf16[1024,128]{1,0:T(8,128)(2,1)} %k_hbm.1, ...), custom_call_target="tpu_custom_call" | custom-call | tf_op jit(solution)/shard_map/attn_grad/pallas_call | solution.py:603
  159.4 0.0 copy-start.1
  159.5 2.2 %copy.12 = bf16[1024,2,128]{2,1,0:T(2,128)(2,1)} copy(bf16[1024,2,128]{2,1,0:T(2,128)(2,1)} %bitcast.5) | data formatting | bytes 1048576
  161.7 0.0 copy-done.1
  161.7 0.0 copy-start
  161.7 0.7 copy.13
  162.4 0.3 copy-done
  162.7 0.7 copy.14
Async XLA Ops:
  159.4 2.2 %copy-start.1 = (bf16[1024,128]{1,0:T(8,128)(2,1)S(1)}, bf16[1024,128]{1,0:T(8,128)(2,1)}, u32[]{:S(2)}) copy-start(bf16[1024,128]{1,0:T(8,128)(2,1)} %get-tuple-element.13) | copy-start | bytes 786436
  161.7 1.0 copy-start
